TPU v7x, 16 devices: a whole 2x2x2 slice. The times are simulated.
16 devices in a mesh: nodes: 16 (over z, y, x, core).
Axes of the slice: x: 2, y: 2, z: 2, core: 2. Of those that a mesh axis runs over, the one named last changes fastest.
Arguments:
- adjacency: bfloat16 [16384, 16384], P('nodes')
- features: bfloat16 [16384, 100], P('nodes')
- w_one: float32 [100, 256], replicated
- w_two: float32 [256, 47], replicated
- labels: int32 [16384], P('nodes')
- label_mask: int32 [16384], P('nodes')
Outputs:
- output 1: float32 [1], replicated
- output 2: float32 [100, 256], replicated
- output 3: float32 [256, 47], replicated
All inputs are finite; a program needn't handle non-finite values.
Results may differ from a plain program's by a relative error of at most 0.001.
Values are sent between devices in bfloat16 or wider.
A program may use at most 1 GiB of HBM per device.

v0:
```python
import jax
import jax.numpy as jnp
from jax import lax
from jax.sharding import PartitionSpec as P

ROW_CONTRACT = (((0,), (0,)), ((), ()))
COL_CONTRACT = (((1,), (1,)), ((), ()))


def solution(mesh):
    axis_name = 'nodes'

    def local_step(adj_rows, feat_rows, w_one, w_two, label_rows, mask_rows):
        weight_one = w_one.astype(jnp.bfloat16)
        weight_two = w_two.astype(jnp.bfloat16)
        num_classes = w_two.shape[1]
        feats_all = lax.all_gather(feat_rows, axis_name, tiled=True)
        agg_one = jnp.dot(adj_rows, feats_all, preferred_element_type=jnp.float32).astype(jnp.bfloat16)
        pre_one = jnp.dot(agg_one, weight_one, preferred_element_type=jnp.float32)
        hidden = jnp.maximum(pre_one, 0.0).astype(jnp.bfloat16)
        hidden_all = lax.all_gather(hidden, axis_name, tiled=True)
        agg_two = jnp.dot(adj_rows, hidden_all, preferred_element_type=jnp.float32).astype(jnp.bfloat16)
        logits = jnp.dot(agg_two, weight_two, preferred_element_type=jnp.float32)
        weight = mask_rows.astype(jnp.float32)
        label_count = lax.psum(jnp.sum(weight), axis_name)
        onehot = (label_rows[:, None] == jnp.arange(num_classes)[None, :]).astype(jnp.float32)
        log_prob = jax.nn.log_softmax(logits, axis=-1)
        loss_sum = lax.psum(-jnp.sum(weight * jnp.sum(onehot * log_prob, axis=-1)), axis_name)
        grad_two = (weight[:, None] * (jnp.exp(log_prob) - onehot) / label_count).astype(jnp.bfloat16)
        dw_two = lax.psum(lax.dot_general(agg_two, grad_two, ROW_CONTRACT, preferred_element_type=jnp.float32), axis_name)
        back_two = lax.dot_general(grad_two, weight_two, COL_CONTRACT, preferred_element_type=jnp.float32).astype(jnp.bfloat16)
        part_sums = lax.dot_general(adj_rows, back_two, ROW_CONTRACT, preferred_element_type=jnp.float32)
        d_hidden = lax.psum_scatter(part_sums, axis_name, scatter_dimension=0, tiled=True)
        grad_one = jnp.where(pre_one > 0.0, d_hidden, 0.0).astype(jnp.bfloat16)
        dw_one = lax.psum(lax.dot_general(agg_one, grad_one, ROW_CONTRACT, preferred_element_type=jnp.float32), axis_name)
        return ((loss_sum / label_count).reshape(1), dw_one, dw_two)

    return jax.shard_map(local_step, mesh=mesh, in_specs=(P(axis_name, None), P(axis_name, None), P(None, None), P(None, None), P(axis_name), P(axis_name)), out_specs=(P(None), P(None, None), P(None, None)), check_vma=False)
```

profile of v0, /device:TPU:0, one launch (start us, length us, event | category | flops | bytes accessed | tf_op | source)
XLA Modules:
  0.0 447.8 jit_solution(2307976300557608291)
XLA Ops:
  7.2 0.0 copy-start.2
  7.2 0.0 copy-start.3
  7.2 0.0 all-gather.3.cloned.1.call-start
  7.2 0.7 all-gather.3.cloned.1.call-update
  7.9 0.0 all-gather.5.cloned.1.call-start
  8.0 38.7 %all-gather.3.cloned.1.call-done = bf16[16384,100]{0,1:T(8,128)(2,1)} async-done(((bf16[1024,100]{0,1:T(8,128)(2,1)}), bf16[16384,100]{0,1:T(8,128)(2,1)}) %all-gather.3.cloned.1.call-update) | async-done | bytes 3276816 | tf_op jit(solution)/shard_map/all_gather | solution.py:17
  46.7 22.0 %convolution_convert_fusion.2 = bf16[1024,100]{0,1:T(8,128)(2,1)S(1)} fusion(bf16[1024,16384]{1,0:T(8,128)(2,1)} %param.6, bf16[16384,100]{0,1:T(8,128)(2,1)} %all-gather.3.cloned.1.call-done), kind=kOutput, calls=%fused_computation.3 | convolution fusion | flops 3355545600 | bytes 37036032 | tf_op jit(solution)/shard_map/dot_general | solution.py:18
  68.7 0.0 copy-done.2
  68.7 1.2 maximum_convert_fusion
  69.9 0.0 all-gather.5.cloned.1.call-update
  70.0 0.0 reduce-scatter.2.cloned.1.call-start
  70.0 0.0 copy-done.3
  70.0 0.0 copy-start
  70.0 0.0 copy-start.1
  70.1 48.7 %all-gather.5.cloned.1.call-done = bf16[16384,256]{1,0:T(8,128)(2,1)} async-done(((bf16[1024,256]{1,0:T(8,128)(2,1)}), bf16[16384,256]{1,0:T(8,128)(2,1)}) %all-gather.5.cloned.1.call-update) | async-done | bytes 8388624 | tf_op jit(solution)/shard_map/all_gather | solution.py:21
  118.8 16.6 %convolution_convert_fusion.1 = bf16[256,1024]{1,0:T(8,128)(2,1)S(1)} fusion(bf16[16384,256]{1,0:T(8,128)(2,1)} %all-gather.5.cloned.1.call-done, bf16[1024,16384]{1,0:T(8,128)(2,1)} %param.6), kind=kOutput, calls=%fused_computation.2 | convolution fusion | flops 8590196736 | bytes 42467328 | tf_op jit(solution)/shard_map/dot_general | solution.py:22
  135.4 0.0 copy-done
  135.4 0.2 fusion.10
  135.7 0.0 copy-done.1
  135.8 0.6 convert_reduce_fusion
  136.4 32.1 %psum.29 = f32[]{:T(128)} all-reduce(f32[]{:T(128)} %get-tuple-element.3), channel_id=1, replica_groups=mesh['nodes'=16] {'nodes'}, use_global_device_ids=true, to_apply=%region_6.7 | all-reduce | flops 1 | bytes 8 | tf_op jit(solution)/shard_map/psum | solution.py:25
  168.4 23.9 %convolution_bitcast_fusion = f32[16384,256]{1,0:T(8,128)} fusion(bf16[1024,16384]{1,0:T(8,128)(2,1)} %param.6, f32[256,47]{0,1:T(8,128)S(1)} %copy-done, f32[1024,47]{0,1:T(8,128)S(1)} %get-tuple-element.10, f32[]{:T(128)} %psum.29, f32[1024]{0:T(1024)S(1)} %convert_element_type.31, f32[1024]{0:T(1024)S(1)} %log.9, f32[1024]{0:T(1024)S(1)} %get-tuple-element.9, ...), kind=kOutput, calls=%fused_computation | convolution fusion | flops 8615235584 | bytes 50588676 | tf_op jit(solution)/shard_map/dot_general | solution.py:32
  192.4 0.0 reduce-scatter.2.cloned.1.call-update
  192.4 0.0 all-reduce.3.cloned.1.call-start
  192.4 178.2 %reduce-scatter.2.cloned.1.call-done = f32[1024,256]{1,0:T(8,128)} async-done(((f32[16384,256]{1,0:T(8,128)}), f32[1024,256]{1,0:T(8,128)}) %reduce-scatter.2.cloned.1.call-update) | async-done | bytes 1048592 | tf_op jit(solution)/shard_map/reduce_scatter | solution.py:33
  370.7 2.1 fusion
  372.8 0.0 all-reduce.3.cloned.1.call-update
  372.8 0.9 fusion.9
  374.4 32.1 %all-reduce = (f32[]{:T(128)}, f32[256,47]{0,1:T(8,128)}) all-reduce(f32[]{:T(128)S(6)} %neg.3, f32[256,47]{0,1:T(8,128)S(1)} %fusion.9), channel_id=1, replica_groups=mesh['nodes'=16] {'nodes'}, use_global_device_ids=true, to_apply=%region_4.5 | all-reduce | flops 12033 | bytes 96264 | tf_op jit(solution)/shard_map/psum | solution.py:28
  407.9 30.7 %all-reduce.3.cloned.1.call-done = f32[100,256]{1,0:T(8,128)} async-done(((f32[100,256]{1,0:T(8,128)}), f32[100,256]{1,0:T(8,128)}) %all-reduce.3.cloned.1.call-update) | async-done | bytes 102416 | tf_op jit(solution)/shard_map/psum | solution.py:35
  438.6 1.5 copy.10
  (4 shorter events, 0.1 us)
Async XLA Ops:
  7.2 61.6 %copy-start.2 = (f32[100,256]{1,0:T(8,128)S(1)}, f32[100,256]{1,0:T(8,128)}, u32[]{:S(2)}) copy-start(f32[100,256]{1,0:T(8,128)} %param.8) | copy-start | bytes 307204
  7.2 62.8 %copy-start.3 = (s32[1024]{0:T(1024)S(1)}, s32[1024]{0:T(1024)}, u32[]{:S(2)}) copy-start(s32[1024]{0:T(1024)} %param.11) | copy-start | bytes 12292
  7.2 39.5 %all-gather.3.cloned.1.call-start = ((), (), s32[]{:S(2)}) async-start(), calls=%async_computation.1 | async-start | bytes 3620864 | tf_op jit(solution)/shard_map/all_gather | solution.py:17
  7.9 110.8 %all-gather.5.cloned.1.call-start = ((), (), s32[]{:S(2)}) async-start(), calls=%async_computation.2 | async-start | bytes 8912896 | tf_op jit(solution)/shard_map/all_gather | solution.py:21
  70.0 300.7 %reduce-scatter.2.cloned.1.call-start = ((), (), s32[]{:S(2)}) async-start(), calls=%async_computation.3 | async-start | bytes 17825792 | tf_op jit(solution)/shard_map/reduce_scatter | solution.py:33
  70.0 65.4 %copy-start = (f32[256,47]{0,1:T(8,128)S(1)}, f32[256,47]{0,1:T(8,128)}, u32[]{:S(2)}) copy-start(f32[256,47]{0,1:T(8,128)} %param.9) | copy-start | bytes 144388
  70.0 65.7 %copy-start.1 = (s32[1024]{0:T(1024)S(1)}, s32[1024]{0:T(1024)}, u32[]{:S(2)}) copy-start(s32[1024]{0:T(1024)} %param.10) | copy-start | bytes 12292
  192.4 246.2 %all-reduce.3.cloned.1.call-start = ((), (), s32[]{:S(2)}) async-start(), calls=%async_computation.4 | async-start | bytes 212992 | tf_op jit(solution)/shard_map/psum | solution.py:35
Sparse Core Ops, SparseCore 0:
  10.3 36.3 all-gather.2
  70.1 48.6 all-gather.4
  192.5 178.1 reduce-scatter.1
  375.3 63.2 all-reduce.2
where the time goes:
time: 448 us
  waiting for transfers between devices  297 us (66%)
  matrix products  67.1 us (15%)
  blocking collectives  64.2 us (14%)
  between operations  17 us (4%)
    reduce_scatter x1, waiting for transfers between devices, local_step(): lax.psum_scatter(part_sums, axis_name, scatter_dimension=0, tiled=True)  178 us
    all_gather x1, waiting for transfers between devices, local_step(): hidden_all = lax.all_gather(hidden, axis_name, tiled=True)  48.7 us
    all_gather x1, waiting for transfers between devices, local_step(): feats_all = lax.all_gather(feat_rows, axis_name, tiled=True)  38.7 us
    psum x1, blocking collectives, local_step(): lax.psum(-jnp.sum(weight * jnp.sum(onehot * log_prob, axis=-1)), axis_name)  32.1 us
    psum x1, blocking collectives, local_step(): label_count = lax.psum(jnp.sum(weight), axis_name)  32.1 us
    psum x1, waiting for transfers between devices, local_step(): lax.psum(lax.dot_general(agg_one, grad_one, ROW_CONTRACT, preferred_eleme...  30.7 us
    dot_general x1, matrix products, local_step(): lax.dot_general(adj_rows, back_two, ROW_CONTRACT, preferred_element_type=...  23.9 us
    dot_general x1, matrix products, local_step(): jnp.dot(adj_rows, feats_all, preferred_element_type=jnp.float32)  22 us
  transfers between devices with their start and end apart: 4, of which 4 were waited for; matrix products, arithmetic and copies ran while one was open for 0% of the time, Pallas kernels for 0%

commit v1 on v0

v1 whole, which is shorter than its diff:
```python
import functools

import jax
import jax.numpy as jnp
from jax import lax
from jax.experimental import pallas as pl
from jax.experimental.pallas import tpu as pltpu
from jax.sharding import PartitionSpec as P

MESH = pl.DeviceIdType.MESH
AXIS = 'nodes'
F32, BF16 = jnp.float32, jnp.bfloat16
NDEV = 16
BLK = 1024
FIN, FPAD = 100, 128
HID = 256
NCLS, CPAD = 47, 48
RING = 4

ORDER = ((0, 1, 2), (1, 2, 0), (2, 0, 1))
GATHER_ROWS = ((0, 352), (352, 336), (688, 336))
REDUCE_ROWS = ((0, 88), (88, 88), (176, 80))

NT = (((1,), (1,)), ((), ()))


def gather_unit(axis, slot):
    first, second, third = axis, (axis + 2) % 3, (axis + 1) % 3
    if slot == 0:
        return first, 0
    if slot == 1:
        return second, 0
    if slot == 2:
        return third, 0
    if slot == 3:
        return second, 1 << ORDER[second][0]
    one, two = 1 << ORDER[third][0], 1 << ORDER[third][1]
    return third, {4: one, 5: two, 6: one | two}[slot]


def reduce_unit(part, k):
    b1, b2, b3 = ORDER[part]
    m1, m2, m3 = 1 << b1, 1 << b2, 1 << b3
    return ((b1, m1 | m2 | m3), (b1, m1 | m2), (b1, m1 | m3), (b1, m1), (b2, m2 | m3), (b2, m2), (b3, m3))[k]


def step_order(i):
    t, j = (i + 1) // 3, (i + 1) % 3
    power = (j * j + j + 2) // 2
    late = t // 5
    one = (1 - t // 3) * ((t + 1) // 2)
    two = (t // 3) * (1 - late)
    zero = 1 - (t + 4) // 5
    mask = one * power + two * (7 - power) + late * 7
    core = zero * (j - 1) + (one + two) * ((t + 1) % 2) + late * j
    return mask, core


def flip(bit, by):
    return bit + by - 2 * bit * by


def kernel(a_hbm, x_hbm, w1_ref, w2_ref, y_ref, m_ref, loss_ref, dw1_ref, dw2_ref,
           abuf, xin, xall, hall, s1acc, s2acc, s1b, s2b, z1t, w1p, w1t, w2p, w2t, ut, acc, drecv, rbuf, gt,
           cnt, d2src, d2r1, d2r2, d1src, d1r1, d1r2,
           asem, xsem, gs, gr, ds, dr, rs, rr, es, er, ms, mr, ps, pr):
    me = lax.axis_index(AXIS)
    core, px, py, pz = me % 2, (me // 2) % 2, (me // 4) % 2, me // 8

    def dev(mask, other=0):
        fx, fy, fz, fc = mask % 2, (mask // 2) % 2, mask // 4, other
        return ((flip(pz, fz) * 2 + flip(py, fy)) * 2 + flip(px, fx)) * 2 + flip(core, fc)

    def block_of(i):
        mask, other = step_order(i)
        return dev(mask, other)

    def load_a(i, slot):
        start = pl.multiple_of(block_of(i) * BLK, BLK)
        return pltpu.make_async_copy(a_hbm.at[:, pl.ds(start, BLK)], abuf.at[slot], asem.at[slot])

    def wait_a(slot):
        pltpu.make_async_copy(a_hbm.at[:, pl.ds(0, BLK)], abuf.at[slot], asem.at[slot]).wait()

    def remote(src, dst, send, recv, to):
        return pltpu.make_async_remote_copy(src_ref=src, dst_ref=dst, send_sem=send, recv_sem=recv,
                                            device_id=(to,), device_id_type=MESH)

    def peer(d):
        return dev(d // 2, d % 2)

    far_first = sorted(range(1, NDEV), key=lambda d: -bin(d // 2).count('1'))

    x_load = pltpu.make_async_copy(x_hbm, xin, xsem.at[0])
    x_load.start()
    for i in range(RING):
        load_a(i, i).start()
    barrier = pltpu.get_barrier_semaphore()
    for d in far_first:
        pl.semaphore_signal(barrier, inc=1, device_id=(peer(d),), device_id_type=MESH)
    w1p[...] = jnp.zeros_like(w1p)
    w1p[0:FIN, :] = w1_ref[...]
    w2p[...] = jnp.zeros_like(w2p)
    w2p[:, 0:NCLS] = w2_ref[...]
    s1acc[...] = jnp.zeros_like(s1acc)
    s2acc[...] = jnp.zeros_like(s2acc)
    xall[me] = jnp.zeros((BLK, FPAD), BF16)
    x_load.wait()
    xall[me, :, 0:FIN] = xin[...]
    cnt[me] = jnp.full((8, 128), jnp.sum(m_ref[...].astype(F32)), F32)
    pl.semaphore_wait(barrier, NDEV - 1)

    def gather(buf, g):
        def copy(axis, slot, at_receiver=False):
            part, mask = gather_unit(axis, slot)
            owner = dev(mask | (1 << axis) if at_receiver else mask)
            ref = buf.at[owner, pl.ds(*GATHER_ROWS[part])]
            n = g * 21 + axis * 7 + slot
            return remote(ref, ref, gs.at[n], gr.at[n], dev(1 << axis))

        def pair(mask, at_receiver=False):
            ref = buf.at[dev(mask, 1 if at_receiver else 0)]
            return remote(ref, ref, ds.at[g * 8 + mask], dr.at[g * 8 + mask], dev(0, 1))

        def begin():
            for slot in range(3):
                for axis in range(3):
                    copy(axis, slot).start()
            pair(0).start()

        def arrive(slots):
            for slot in slots:
                for axis in range(3):
                    copy(axis, slot, True).wait_recv()
                    part, mask = gather_unit(axis, slot)
                    got = (part, mask | (1 << axis))
                    for later in range(3, 7):
                        for onto in range(3):
                            if gather_unit(onto, later) == got:
                                copy(onto, later).start()

        def hooks(i):
            @pl.when(i == 1)
            def _():
                pair(0, True).wait_recv()

            @pl.when(i == 2)
            def _():
                arrive((0, 1, 2))
                for mask in (1, 2, 4):
                    pair(mask).start()

            @pl.when(i == 8)
            def _():
                arrive((3, 4, 5))
                for mask in (6, 5, 3):
                    pair(mask).start()

            @pl.when(i == 14)
            def _():
                arrive((6,))
                pair(7).start()

            for step in (5, 6, 7, 11, 12, 13, 15):
                @pl.when(i == step)
                def _():
                    pair(step_order(step)[0], True).wait_recv()

        def drain():
            for axis in range(3):
                for slot in range(7):
                    copy(axis, slot).wait_send()
            for mask in range(8):
                pair(mask).wait_send()

        return begin, hooks, drain

    def aggregate(buf, total, hooks, g):
        @pl.loop(0, NDEV)
        def _(i):
            hooks(i)
            slot = i % RING
            wait_a(slot)
            block = block_of(i)

            @pl.loop(0, 2)
            def _(half):
                rows = pl.ds(pl.multiple_of(half * 512, 512), 512)
                total[rows, :] += jnp.dot(abuf[slot, rows, :], buf[block], preferred_element_type=F32)

            if g == 0:
                load_a((i + RING) % NDEV, slot).start()
            else:
                @pl.when(i < NDEV - RING)
                def _():
                    load_a(i + RING, slot).start()

    def count_copy(d):
        ref = cnt.at[me]
        return remote(ref, ref, ms.at[d], mr.at[d], peer(d))

    begin_x, hooks_x, drain_x = gather(xall, 0)
    begin_h, hooks_h, drain_h = gather(hall, 1)

    begin_x()
    for d in far_first:
        count_copy(d).start()
    w1t[...] = w1p[...].T.astype(BF16)
    w2t[...] = w2p[...].T.astype(BF16)
    aggregate(xall, s1acc, hooks_x, 0)

    s1b[...] = s1acc[...].astype(BF16)
    pre_one = jnp.dot(s1b[...], w1p[...].astype(BF16), preferred_element_type=F32)
    hall[me] = jnp.maximum(pre_one, 0.0).astype(BF16)
    z1t[...] = lax.dot_general(w1t[...], s1b[...], NT, preferred_element_type=F32)
    begin_h()
    aggregate(hall, s2acc, hooks_h, 1)

    for d in range(1, NDEV):
        ref = cnt.at[peer(d)]
        remote(ref, ref, ms.at[d], mr.at[d], peer(d)).wait_recv()
    label_count = jnp.sum(cnt[...], axis=0)[0:1, 0:1]
    s2b[...] = s2acc[...].astype(BF16)
    logits = lax.dot_general(w2t[...], s2b[...], NT, preferred_element_type=F32)[0:CPAD]
    classes = lax.broadcasted_iota(jnp.int32, (CPAD, BLK), 0)
    logits = jnp.where(classes < NCLS, logits, -jnp.inf)
    shifted = logits - jnp.max(logits, axis=0, keepdims=True)
    log_prob = shifted - jnp.log(jnp.sum(jnp.exp(shifted), axis=0, keepdims=True))
    hit = classes == y_ref[...]
    weight = m_ref[...].astype(F32)
    picked = jnp.sum(jnp.where(hit, log_prob, 0.0), axis=0, keepdims=True)
    loss_part = -jnp.sum(weight * picked)
    grad = weight * (jnp.exp(log_prob) - jnp.where(hit, 1.0, 0.0)) / label_count
    gt[...] = grad.astype(BF16)
    ut[...] = jnp.dot(w2p[...][:, 0:CPAD].astype(BF16), gt[...], preferred_element_type=F32).astype(BF16)

    def pair_sum(mask):
        return remote(acc.at[8 + mask], drecv.at[mask], es.at[mask], er.at[mask], dev(0, 1))

    def unit_copy(part, k):
        axis, mask = reduce_unit(part, k)
        rows = pl.ds(*REDUCE_ROWS[part])
        n = part * 7 + k
        return remote(acc.at[mask, rows], rbuf.at[k, rows], rs.at[n], rr.at[n], dev(1 << axis))

    def add_rows(mask, source, start, size):
        @pl.loop(0, size // 8)
        def _(t):
            rows = pl.ds(pl.multiple_of(start + t * 8, 8), 8)
            acc[mask, rows, :] += source[rows, :]

    def take_pair(mask):
        pair_sum(mask).wait_recv()
        add_rows(mask, drecv.at[mask], 0, HID)
        for k in range(4):
            for part in range(3):
                if reduce_unit(part, k)[1] == mask:
                    unit_copy(part, k).start()

    @pl.loop(0, NDEV)
    def _(i):
        slot = (NDEV - 1 - i) % RING
        mask, other = step_order(NDEV - 1 - i)

        @pl.when(i >= RING)
        def _():
            wait_a(slot)

        @pl.loop(0, 2)
        def _(half):
            cols = pl.ds(pl.multiple_of(half * 512, 512), 512)
            acc[mask + 8 * other, :, cols] = jnp.dot(ut[...], abuf[slot, :, cols], preferred_element_type=F32)

        @pl.when(i < NDEV - RING)
        def _():
            load_a(NDEV - 1 - i - RING, slot).start()

        for step in range(NDEV):
            step_mask, step_other = step_order(NDEV - 1 - step)

            @pl.when(i == step)
            def _():
                if step_other:
                    pair_sum(step_mask).start()
                else:
                    take_pair(step_mask)

    def small_scatter(src, dst, d, base, wait):
        if wait:
            ref = dst.at[peer(d)]
            return remote(ref, ref, ps.at[base + d], pr.at[base + d], peer(d))
        return remote(src.at[peer(d)], dst.at[me], ps.at[base + d], pr.at[base + d], peer(d))

    def small_gather(dst, d, base, wait):
        ref = dst.at[peer(d)] if wait else dst.at[me]
        return remote(ref, ref, ps.at[base + d], pr.at[base + d], peer(d))

    dw2_part = jnp.dot(gt[...], s2b[...], preferred_element_type=F32)
    d2src[...] = jnp.zeros_like(d2src)
    for j in range(6):
        d2src[j] = dw2_part[j * 8:(j + 1) * 8, 0:128]
        d2src[6 + j] = dw2_part[j * 8:(j + 1) * 8, 128:256]
    d2src[12] = jnp.full((8, 128), loss_part, F32)
    d2r1[me] = d2src[me]
    for d in far_first:
        small_scatter(d2src, d2r1, d, 0, False).start()

    def take_unit(part, k, send=None):
        axis, mask = reduce_unit(part, k)
        unit_copy(part, k).wait_recv()
        add_rows(mask - (1 << axis), rbuf.at[k], *REDUCE_ROWS[part])
        if send is not None:
            unit_copy(part, send).start()

    for part in range(3):
        take_unit(part, 0, 4)
    for part in range(3):
        take_unit(part, 1, 5)
    for part in range(3):
        take_unit(part, 2)
    for d in range(1, NDEV):
        small_scatter(d2src, d2r1, d, 0, True).wait_recv()
    d2r2[me] = jnp.sum(d2r1[...], axis=0)
    for d in far_first:
        small_gather(d2r2, d, 16, False).start()
    for part in range(3):
        take_unit(part, 3)
    for part in range(3):
        take_unit(part, 4, 6)
    for part in range(3):
        take_unit(part, 5)
    for part in range(3):
        take_unit(part, 6)

    grad_one = jnp.where(z1t[...] > 0.0, acc[0], 0.0).astype(BF16)
    d1src[...] = jnp.dot(grad_one, s1b[...], preferred_element_type=F32).reshape(NDEV, 16, FPAD)
    d1r1[me] = d1src[me]
    for d in far_first:
        small_scatter(d1src, d1r1, d, 32, False).start()
    for d in range(1, NDEV):
        small_gather(d2r2, d, 16, True).wait_recv()
    left = d2r2[0:6].reshape(CPAD, 128)
    right = d2r2[6:12].reshape(CPAD, 128)
    dw2_ref[:, :] = jnp.concatenate([left, right], axis=1).T[:, 0:NCLS]
    loss_ref[...] = d2r2[12] / label_count
    for d in range(1, NDEV):
        small_scatter(d1src, d1r1, d, 32, True).wait_recv()
    d1r2[me] = jnp.sum(d1r1[...], axis=0)
    for d in far_first:
        small_gather(d1r2, d, 48, False).start()
    drain_x()
    drain_h()
    for mask in range(8):
        pair_sum(mask).wait_send()
    for part in range(3):
        for k in range(7):
            unit_copy(part, k).wait_send()
    for d in range(1, NDEV):
        count_copy(d).wait_send()
        small_scatter(d2src, d2r1, d, 0, False).wait_send()
        small_gather(d2r2, d, 16, False).wait_send()
        small_scatter(d1src, d1r1, d, 32, False).wait_send()
    for d in range(1, NDEV):
        small_gather(d1r2, d, 48, True).wait_recv()
    dw1_ref[...] = d1r2[...].reshape(HID, FPAD).T[0:FIN, :]
    for d in range(1, NDEV):
        small_gather(d1r2, d, 48, False).wait_send()


def solution(mesh):
    def local_step(adj_rows, feat_rows, w_one, w_two, label_rows, mask_rows):
        vmem = pl.BlockSpec(memory_space=pltpu.VMEM)
        hbm = pl.BlockSpec(memory_space=pl.ANY)
        dma = pltpu.SemaphoreType.DMA
        loss, dw_one, dw_two = pl.pallas_call(
            kernel,
            out_shape=(jax.ShapeDtypeStruct((8, 128), F32), jax.ShapeDtypeStruct((FIN, HID), F32),
                       jax.ShapeDtypeStruct((HID, NCLS), F32)),
            in_specs=[hbm, hbm, vmem, vmem, vmem, vmem],
            out_specs=(vmem, vmem, vmem),
            scratch_shapes=[
                pltpu.VMEM((RING, BLK, BLK), BF16),
                pltpu.VMEM((BLK, FIN), BF16),
                pltpu.VMEM((NDEV, BLK, FPAD), BF16),
                pltpu.VMEM((NDEV, BLK, HID), BF16),
                pltpu.VMEM((BLK, FPAD), F32),
                pltpu.VMEM((BLK, HID), F32),
                pltpu.VMEM((BLK, FPAD), BF16),
                pltpu.VMEM((BLK, HID), BF16),
                pltpu.VMEM((HID, BLK), F32),
                pltpu.VMEM((FPAD, HID), F32),
                pltpu.VMEM((HID, FPAD), BF16),
                pltpu.VMEM((HID, 128), F32),
                pltpu.VMEM((128, HID), BF16),
                pltpu.VMEM((HID, BLK), BF16),
                pltpu.VMEM((16, HID, BLK), F32),
                pltpu.VMEM((8, HID, BLK), F32),
                pltpu.VMEM((7, HID, BLK), F32),
                pltpu.VMEM((CPAD, BLK), BF16),
                pltpu.VMEM((NDEV, 8, 128), F32),
                pltpu.VMEM((NDEV, 8, 128), F32),
                pltpu.VMEM((NDEV, 8, 128), F32),
                pltpu.VMEM((NDEV, 8, 128), F32),
                pltpu.VMEM((NDEV, 16, FPAD), F32),
                pltpu.VMEM((NDEV, 16, FPAD), F32),
                pltpu.VMEM((NDEV, 16, FPAD), F32),
                dma((RING,)), dma((1,)), dma((42,)), dma((42,)), dma((16,)), dma((16,)), dma((21,)), dma((21,)),
                dma((8,)), dma((8,)), dma((16,)), dma((16,)), dma((64,)), dma((64,)),
            ],
            compiler_params=pltpu.CompilerParams(collective_id=0, has_side_effects=True,
                                                 vmem_limit_bytes=66 * 1000 * 1000),
        )(adj_rows, feat_rows, w_one, w_two, label_rows.reshape(1, BLK), mask_rows.reshape(1, BLK))
        return loss[0, 0:1], dw_one, dw_two

    return jax.shard_map(local_step, mesh=mesh,
                         in_specs=(P(AXIS, None), P(AXIS, None), P(None, None), P(None, None), P(AXIS), P(AXIS)),
                         out_specs=(P(None), P(None, None), P(None, None)), check_vma=False)
```

time: 448 us -> 145 us (0.32)
  waiting for transfers between devices: 297 us -> 0 us
  Pallas kernels: 0 us -> 136 us
  matrix products: 67.1 us -> 0 us
  blocking collectives: 64.2 us -> 0 us
  between operations: 17 us -> 0.64 us
  local copies, waits for them, and re-layouts: 1.57 us -> 7.67 us
    reduce_scatter x1 -> x0, waiting for transfers between devices: 178 us -> none  [local_step(): lax.psum_scatter(part_sums, axis_name, scatter_dimension=0, tiled=True)]
    pallas_call x0 -> x1, Pallas kernels: none -> 136 us  [local_step(): pl.pallas_call(kernel, out_shape=(jax.ShapeDtypeStruct((8, 128), F32), ja...]
    all_gather x2 -> x0, waiting for transfers between devices: 87.4 us -> none  [the longest x1 48.7 us: local_step(): hidden_all = lax.all_gather(hidden, axis_name, tiled=True)]
    dot_general x7 -> x0, matrix products: 67.1 us -> none  [the longest x1 23.9 us: local_step(): lax.dot_general(adj_rows, back_two, ROW_CONTRACT, preferred_element_type=...]
    psum x2 -> x0, blocking collectives: 64.2 us -> none  [the longest x1 32.1 us: local_step(): lax.psum(-jnp.sum(weight * jnp.sum(onehot * log_prob, axis=-1)), axis_name)]
    psum x1 -> x0, waiting for transfers between devices: 30.7 us -> none  [local_step(): lax.psum(lax.dot_general(agg_one, grad_one, ROW_CONTRACT, preferred_eleme...]
    unnamed x9 -> x4, local copies, waits for them, and re-layouts: 1.57 us -> 6.49 us
  transfers between devices with their start and end apart: 4 -> 0, of which waited for: 4 -> 0; matrix products, arithmetic and copies ran while one was open for 0% -> 0% of each run, Pallas kernels for 0% -> 0%
where the time goes in v1:
time: 145 us
  Pallas kernels  136 us (94%)
  local copies, waits for them, and re-layouts  7.67 us (5%)
    pallas_call x1, Pallas kernels, local_step(): pl.pallas_call(kernel, out_shape=(jax.ShapeDtypeStruct((8, 128), F32), ja...  136 us
    unnamed x4, local copies, waits for them, and re-layouts  6.49 us

profile of v1, /device:TPU:0, one launch (start us, length us, event | category | flops | bytes accessed | tf_op | source)
XLA Modules:
  0.0 144.8 jit_solution(2389644669993550988)
XLA Ops:
  0.6 1.6 %copy.10.w2_ref = f32[256,47]{1,0:T(8,128)} copy(f32[256,47]{0,1:T(8,128)} %param.9) | data formatting | bytes 96256 | tf_op args[3]
  2.2 1.8 %copy.9.x_hbm = bf16[1024,100]{1,0:T(8,128)(2,1)} copy(bf16[1024,100]{0,1:T(8,128)(2,1)} %param.7) | data formatting | bytes 409600 | tf_op args[1]
  4.0 136.5 %shard_map.85 = (f32[8,128]{1,0:T(8,128)}, f32[100,256]{1,0:T(8,128)}, f32[256,47]{1,0:T(8,128)}) custom-call(bf16[1024,16384]{1,0:T(8,128)(2,1)} %a_hbm.1, bf16[1024,100]{1,0:T(8,128)(2,1)} %copy.9.x_hbm, f32[100,256]{1,0:T(8,128)} %w1_ref.1, f32[256,47]{1,0:T(8,128)} %copy.10.w2_ref, s32[1,1024]{1,0:T(1,128)} %bitcast.3, s32[1,1024]{1,0:T(1,128)} %bitcast.4), custom_call_target="tpu_custom_call" | custom-call | tf_op jit(solution)/shard_map/pallas_call | solution.py:375
  140.5 1.2 slice.3
  141.6 1.6 %copy.11 = f32[256,47]{0,1:T(8,128)} copy(f32[256,47]{1,0:T(8,128)} %get-tuple-element.11) | data formatting | bytes 96256
  143.3 1.5 %copy.13 = f32[100,256]{1,0:T(8,128)} copy(f32[100,256]{1,0:T(8,128)} %get-tuple-element.16) | data formatting | bytes 204800

commit v2 on v1

--- a/solution.py
+++ b/solution.py
@@ -12,16 +12,18 @@
 F32, BF16 = jnp.float32, jnp.bfloat16
 NDEV = 16
 BLK = 1024
-FIN, FPAD = 100, 128
+FIN, FROWS, FPAD = 100, 104, 128
 HID = 256
 NCLS, CPAD = 47, 48
 RING = 4
 
 ORDER = ((0, 1, 2), (1, 2, 0), (2, 0, 1))
 GATHER_ROWS = ((0, 352), (352, 336), (688, 336))
+GATHER_COLS = ((0, 384), (384, 384), (768, 256))
 REDUCE_ROWS = ((0, 88), (88, 88), (176, 80))
 
 NT = (((1,), (1,)), ((), ()))
+TN = (((0,), (0,)), ((), ()))
 
 
 def gather_unit(axis, slot):
@@ -60,8 +62,9 @@
     return bit + by - 2 * bit * by
 
 
-def kernel(a_hbm, x_hbm, w1_ref, w2_ref, y_ref, m_ref, loss_ref, dw1_ref, dw2_ref,
-           abuf, xin, xall, hall, s1acc, s2acc, s1b, s2b, z1t, w1p, w1t, w2p, w2t, ut, acc, drecv, rbuf, gt,
+def kernel(a_hbm, x_hbm, w1_hbm, w2_hbm, y_hbm, m_hbm, loss_ref, dw1_ref, dw2_ref,
+           abuf, xin, w1_ref, w2_ref, y_ref, m_ref, xall, hall, s1acc, s2acc, s1b, s2b, z1t, w1p, w1t, w2t, ut,
+           acc, drecv, rbuf, gt,
            cnt, d2src, d2r1, d2r2, d1src, d1r1, d1r2,
            asem, xsem, gs, gr, ds, dr, rs, rr, es, er, ms, mr, ps, pr):
     me = lax.axis_index(AXIS)
@@ -91,30 +94,30 @@
 
     far_first = sorted(range(1, NDEV), key=lambda d: -bin(d // 2).count('1'))
 
-    x_load = pltpu.make_async_copy(x_hbm, xin, xsem.at[0])
-    x_load.start()
+    loads = [pltpu.make_async_copy(src, dst, xsem.at[k]) for k, (src, dst) in enumerate((
+        (x_hbm, xin), (m_hbm, m_ref), (w1_hbm, w1_ref), (w2_hbm, w2_ref), (y_hbm, y_ref)))]
+    for load in loads:
+        load.start()
     for i in range(RING):
         load_a(i, i).start()
     barrier = pltpu.get_barrier_semaphore()
     for d in far_first:
         pl.semaphore_signal(barrier, inc=1, device_id=(peer(d),), device_id_type=MESH)
-    w1p[...] = jnp.zeros_like(w1p)
-    w1p[0:FIN, :] = w1_ref[...]
-    w2p[...] = jnp.zeros_like(w2p)
-    w2p[:, 0:NCLS] = w2_ref[...]
-    s1acc[...] = jnp.zeros_like(s1acc)
-    s2acc[...] = jnp.zeros_like(s2acc)
-    xall[me] = jnp.zeros((BLK, FPAD), BF16)
-    x_load.wait()
-    xall[me, :, 0:FIN] = xin[...]
+    xall[me] = jnp.zeros((FROWS, BLK), BF16)
+    loads[0].wait()
+    xall[me, 0:FIN, :] = xin[...]
+    loads[1].wait()
     cnt[me] = jnp.full((8, 128), jnp.sum(m_ref[...].astype(F32)), F32)
     pl.semaphore_wait(barrier, NDEV - 1)
 
     def gather(buf, g):
+        def piece(owner, part):
+            return buf.at[owner, :, pl.ds(*GATHER_COLS[part])] if g == 0 else buf.at[owner, pl.ds(*GATHER_ROWS[part])]
+
         def copy(axis, slot, at_receiver=False):
             part, mask = gather_unit(axis, slot)
             owner = dev(mask | (1 << axis) if at_receiver else mask)
-            ref = buf.at[owner, pl.ds(*GATHER_ROWS[part])]
+            ref = piece(owner, part)
             n = g * 21 + axis * 7 + slot
             return remote(ref, ref, gs.at[n], gr.at[n], dev(1 << axis))
 
@@ -186,7 +189,11 @@
             @pl.loop(0, 2)
             def _(half):
                 rows = pl.ds(pl.multiple_of(half * 512, 512), 512)
-                total[rows, :] += jnp.dot(abuf[slot, rows, :], buf[block], preferred_element_type=F32)
+                if g == 0:
+                    total[0:FROWS, rows] += lax.dot_general(buf[block], abuf[slot, rows, :], NT,
+                                                            preferred_element_type=F32)
+                else:
+                    total[rows, :] += jnp.dot(abuf[slot, rows, :], buf[block], preferred_element_type=F32)
 
             if g == 0:
                 load_a((i + RING) % NDEV, slot).start()
@@ -205,14 +212,21 @@
     begin_x()
     for d in far_first:
         count_copy(d).start()
+    for load in loads[2:]:
+        load.wait()
+    w1p[...] = jnp.zeros_like(w1p)
+    w1p[0:FIN, :] = w1_ref[...]
     w1t[...] = w1p[...].T.astype(BF16)
-    w2t[...] = w2p[...].T.astype(BF16)
+    w2t[...] = jnp.zeros_like(w2t)
+    w2t[0:NCLS, :] = w2_ref[...].astype(BF16)
+    s1acc[...] = jnp.zeros_like(s1acc)
+    s2acc[...] = jnp.zeros_like(s2acc)
     aggregate(xall, s1acc, hooks_x, 0)
 
     s1b[...] = s1acc[...].astype(BF16)
-    pre_one = jnp.dot(s1b[...], w1p[...].astype(BF16), preferred_element_type=F32)
+    pre_one = jnp.dot(s1acc[...].T.astype(BF16), w1p[...].astype(BF16), preferred_element_type=F32)
     hall[me] = jnp.maximum(pre_one, 0.0).astype(BF16)
-    z1t[...] = lax.dot_general(w1t[...], s1b[...], NT, preferred_element_type=F32)
+    z1t[...] = jnp.dot(w1t[...], s1b[...], preferred_element_type=F32)
     begin_h()
     aggregate(hall, s2acc, hooks_h, 1)
 
@@ -221,7 +235,7 @@
         remote(ref, ref, ms.at[d], mr.at[d], peer(d)).wait_recv()
     label_count = jnp.sum(cnt[...], axis=0)[0:1, 0:1]
     s2b[...] = s2acc[...].astype(BF16)
-    logits = lax.dot_general(w2t[...], s2b[...], NT, preferred_element_type=F32)[0:CPAD]
+    logits = lax.dot_general(w2t[...], s2b[...], NT, preferred_element_type=F32)
     classes = lax.broadcasted_iota(jnp.int32, (CPAD, BLK), 0)
     logits = jnp.where(classes < NCLS, logits, -jnp.inf)
     shifted = logits - jnp.max(logits, axis=0, keepdims=True)
@@ -232,7 +246,7 @@
     loss_part = -jnp.sum(weight * picked)
     grad = weight * (jnp.exp(log_prob) - jnp.where(hit, 1.0, 0.0)) / label_count
     gt[...] = grad.astype(BF16)
-    ut[...] = jnp.dot(w2p[...][:, 0:CPAD].astype(BF16), gt[...], preferred_element_type=F32).astype(BF16)
+    ut[...] = lax.dot_general(w2t[...], gt[...], TN, preferred_element_type=F32).astype(BF16)
 
     def pair_sum(mask):
         return remote(acc.at[8 + mask], drecv.at[mask], es.at[mask], er.at[mask], dev(0, 1))
@@ -333,7 +347,7 @@
         take_unit(part, 6)
 
     grad_one = jnp.where(z1t[...] > 0.0, acc[0], 0.0).astype(BF16)
-    d1src[...] = jnp.dot(grad_one, s1b[...], preferred_element_type=F32).reshape(NDEV, 16, FPAD)
+    d1src[...] = lax.dot_general(grad_one, s1b[...], NT, preferred_element_type=F32).reshape(NDEV, 16, FPAD)
     d1r1[me] = d1src[me]
     for d in far_first:
         small_scatter(d1src, d1r1, d, 32, False).start()
@@ -341,7 +355,7 @@
         small_gather(d2r2, d, 16, True).wait_recv()
     left = d2r2[0:6].reshape(CPAD, 128)
     right = d2r2[6:12].reshape(CPAD, 128)
-    dw2_ref[:, :] = jnp.concatenate([left, right], axis=1).T[:, 0:NCLS]
+    dw2_ref[...] = jnp.concatenate([left, right], axis=1)
     loss_ref[...] = d2r2[12] / label_count
     for d in range(1, NDEV):
         small_scatter(d1src, d1r1, d, 32, True).wait_recv()
@@ -362,9 +376,15 @@
         small_scatter(d1src, d1r1, d, 32, False).wait_send()
     for d in range(1, NDEV):
         small_gather(d1r2, d, 48, True).wait_recv()
-    dw1_ref[...] = d1r2[...].reshape(HID, FPAD).T[0:FIN, :]
+    dw1_ref[...] = d1r2[...].reshape(HID, FPAD)
     for d in range(1, NDEV):
         small_gather(d1r2, d, 48, False).wait_send()
+
+
+def finish(loss_ref, dw1_ref, dw2_ref, loss_out, dw1_out, dw2_out):
+    loss_out[...] = loss_ref[0:1, 0:1]
+    dw1_out[...] = dw1_ref[...].T[0:FIN, :]
+    dw2_out[...] = dw2_ref[0:NCLS, :]
 
 
 def solution(mesh):
@@ -372,26 +392,29 @@
         vmem = pl.BlockSpec(memory_space=pltpu.VMEM)
         hbm = pl.BlockSpec(memory_space=pl.ANY)
         dma = pltpu.SemaphoreType.DMA
-        loss, dw_one, dw_two = pl.pallas_call(
+        parts = pl.pallas_call(
             kernel,
-            out_shape=(jax.ShapeDtypeStruct((8, 128), F32), jax.ShapeDtypeStruct((FIN, HID), F32),
-                       jax.ShapeDtypeStruct((HID, NCLS), F32)),
-            in_specs=[hbm, hbm, vmem, vmem, vmem, vmem],
+            out_shape=(jax.ShapeDtypeStruct((8, 128), F32), jax.ShapeDtypeStruct((HID, FPAD), F32),
+                       jax.ShapeDtypeStruct((CPAD, HID), F32)),
+            in_specs=[hbm] * 6,
             out_specs=(vmem, vmem, vmem),
             scratch_shapes=[
                 pltpu.VMEM((RING, BLK, BLK), BF16),
-                pltpu.VMEM((BLK, FIN), BF16),
-                pltpu.VMEM((NDEV, BLK, FPAD), BF16),
+                pltpu.VMEM((FIN, BLK), BF16),
+                pltpu.VMEM((FIN, HID), F32),
+                pltpu.VMEM((NCLS, HID), F32),
+                pltpu.VMEM((1, BLK), jnp.int32),
+                pltpu.VMEM((1, BLK), jnp.int32),
+                pltpu.VMEM((NDEV, FROWS, BLK), BF16),
                 pltpu.VMEM((NDEV, BLK, HID), BF16),
-                pltpu.VMEM((BLK, FPAD), F32),
+                pltpu.VMEM((FPAD, BLK), F32),
                 pltpu.VMEM((BLK, HID), F32),
-                pltpu.VMEM((BLK, FPAD), BF16),
+                pltpu.VMEM((FPAD, BLK), BF16),
                 pltpu.VMEM((BLK, HID), BF16),
                 pltpu.VMEM((HID, BLK), F32),
                 pltpu.VMEM((FPAD, HID), F32),
                 pltpu.VMEM((HID, FPAD), BF16),
-                pltpu.VMEM((HID, 128), F32),
-                pltpu.VMEM((128, HID), BF16),
+                pltpu.VMEM((CPAD, HID), BF16),
                 pltpu.VMEM((HID, BLK), BF16),
                 pltpu.VMEM((16, HID, BLK), F32),
                 pltpu.VMEM((8, HID, BLK), F32),
@@ -404,13 +427,20 @@
                 pltpu.VMEM((NDEV, 16, FPAD), F32),
                 pltpu.VMEM((NDEV, 16, FPAD), F32),
                 pltpu.VMEM((NDEV, 16, FPAD), F32),
-                dma((RING,)), dma((1,)), dma((42,)), dma((42,)), dma((16,)), dma((16,)), dma((21,)), dma((21,)),
+                dma((RING,)), dma((5,)), dma((42,)), dma((42,)), dma((16,)), dma((16,)), dma((21,)), dma((21,)),
                 dma((8,)), dma((8,)), dma((16,)), dma((16,)), dma((64,)), dma((64,)),
             ],
             compiler_params=pltpu.CompilerParams(collective_id=0, has_side_effects=True,
-                                                 vmem_limit_bytes=66 * 1000 * 1000),
-        )(adj_rows, feat_rows, w_one, w_two, label_rows.reshape(1, BLK), mask_rows.reshape(1, BLK))
-        return loss[0, 0:1], dw_one, dw_two
+                                                 vmem_limit_bytes=62 * 1000 * 1000),
+        )(adj_rows, feat_rows.T, w_one, w_two.T, label_rows.reshape(1, BLK), mask_rows.reshape(1, BLK))
+        loss, dw_one, dw_two = pl.pallas_call(
+            finish,
+            out_shape=(jax.ShapeDtypeStruct((1, 1), F32), jax.ShapeDtypeStruct((FIN, HID), F32),
+                       jax.ShapeDtypeStruct((NCLS, HID), F32)),
+            in_specs=[vmem] * 3,
+            out_specs=(vmem, vmem, vmem),
+        )(*parts)
+        return loss.reshape(1), dw_one, dw_two.T
 
     return jax.shard_map(local_step, mesh=mesh,
                          in_specs=(P(AXIS, None), P(AXIS, None), P(None, None), P(None, None), P(AXIS), P(AXIS)),

time: 145 us -> 138 us (0.952)
  local copies, waits for them, and re-layouts: 7.67 us -> 0 us
    unnamed x4 -> x0, local copies, waits for them, and re-layouts: 6.49 us -> none
    pallas_call x0 -> x1, Pallas kernels: none -> 1.66 us  [local_step(): pl.pallas_call(finish, out_shape=(jax.ShapeDtypeStruct((1, 1), F32), jax....]
where the time goes in v2:
time: 138 us
  Pallas kernels  137 us (99%)
    pallas_call x1, Pallas kernels, local_step(): pl.pallas_call(kernel, out_shape=(jax.ShapeDtypeStruct((8, 128), F32), ja...  136 us

profile of v2, /device:TPU:0, one launch (start us, length us, event | category | flops | bytes accessed | tf_op | source)
XLA Modules:
  0.0 137.9 jit_solution(7626791109229953407)
XLA Ops:
  0.6 135.6 %shard_map.85 = (f32[8,128]{1,0:T(8,128)}, f32[256,128]{1,0:T(8,128)}, f32[48,256]{1,0:T(8,128)}) custom-call(bf16[1024,16384]{1,0:T(8,128)(2,1)} %a_hbm.1, bf16[100,1024]{1,0:T(8,128)(2,1)} %bitcast.6, f32[100,256]{1,0:T(8,128)} %w1_hbm.1, f32[47,256]{1,0:T(8,128)} %bitcast.7, s32[1,1024]{1,0:T(1,128)} %bitcast.8, s32[1,1024]{1,0:T(1,128)} %bitcast.9), custom_call_target="tpu_custom_call" | custom-call | tf_op jit(solution)/shard_map/pallas_call | solution.py:395
  136.3 1.7 %shard_map.86 = (f32[1,1]{1,0:T(1,128)}, f32[100,256]{1,0:T(8,128)}, f32[47,256]{1,0:T(8,128)}) custom-call(f32[8,128]{1,0:T(8,128)} %get-tuple-element.9.loss_ref, f32[256,128]{1,0:T(8,128)} %get-tuple-element.10.dw1_ref, f32[48,256]{1,0:T(8,128)} %get-tuple-element.11.dw2_ref), custom_call_target="tpu_custom_call" | custom-call | tf_op jit(solution)/shard_map/pallas_call | solution.py:436

commit v3 on v2

--- a/solution.py
+++ b/solution.py
@@ -15,9 +15,11 @@
 FIN, FROWS, FPAD = 100, 104, 128
 HID = 256
 NCLS, CPAD = 47, 48
-RING = 4
-
-ORDER = ((0, 1, 2), (1, 2, 0), (2, 0, 1))
+RING = 6
+SEMS = 64
+TILE = (8, 128)
+
+ORDER = tuple((p, (p + 1) % 3, (p + 2) % 3) for p in range(3))
 GATHER_ROWS = ((0, 352), (352, 336), (688, 336))
 GATHER_COLS = ((0, 384), (384, 384), (768, 256))
 REDUCE_ROWS = ((0, 88), (88, 88), (176, 80))
@@ -47,14 +49,11 @@
 
 
 def step_order(i):
-    t, j = (i + 1) // 3, (i + 1) % 3
-    power = (j * j + j + 2) // 2
-    late = t // 5
-    one = (1 - t // 3) * ((t + 1) // 2)
-    two = (t // 3) * (1 - late)
-    zero = 1 - (t + 4) // 5
-    mask = one * power + two * (7 - power) + late * 7
-    core = zero * (j - 1) + (one + two) * ((t + 1) % 2) + late * j
+    from2, from8, from10, from14 = ((i + 16 - n) // 16 for n in (2, 8, 10, 14))
+    j = (i + 1) % 3
+    one, xy, two = from2 - from8, from8 - from10, from10 - from14
+    mask = one * ((j * j + j + 2) // 2) + xy * 3 + two * (5 + i % 2) + from14 * 7
+    core = (1 - from2) * i + one * ((i + 1) // 3 - 1) + xy * (i - 8) + two * (i // 2 - 5) + from14 * (i - 14)
     return mask, core
 
 
@@ -101,14 +100,14 @@
     for i in range(RING):
         load_a(i, i).start()
     barrier = pltpu.get_barrier_semaphore()
-    for d in far_first:
+    for d in (8, 4, 2, 1):
         pl.semaphore_signal(barrier, inc=1, device_id=(peer(d),), device_id_type=MESH)
     xall[me] = jnp.zeros((FROWS, BLK), BF16)
     loads[0].wait()
     xall[me, 0:FIN, :] = xin[...]
     loads[1].wait()
-    cnt[me] = jnp.full((8, 128), jnp.sum(m_ref[...].astype(F32)), F32)
-    pl.semaphore_wait(barrier, NDEV - 1)
+    cnt[me] = jnp.full((1, 128), jnp.sum(m_ref[...].astype(F32)), F32)
+    pl.semaphore_wait(barrier, 4)
 
     def gather(buf, g):
         def piece(owner, part):
@@ -122,79 +121,108 @@
             return remote(ref, ref, gs.at[n], gr.at[n], dev(1 << axis))
 
         def pair(mask, at_receiver=False):
-            ref = buf.at[dev(mask, 1 if at_receiver else 0)]
-            return remote(ref, ref, ds.at[g * 8 + mask], dr.at[g * 8 + mask], dev(0, 1))
+            return [pair_piece(mask, k, at_receiver) for k in range(1 if mask < 7 else 3)]
+
+        def pair_piece(mask, k, at_receiver=False):
+            owner = dev(mask, 1 if at_receiver else 0)
+            ref = buf.at[owner] if mask < 7 else piece(owner, k)
+            return remote(ref, ref, ds.at[g * 10 + mask + k], dr.at[g * 10 + mask + k], dev(0, 1))
+
+        def give(*masks):
+            for mask in masks:
+                for c in pair(mask):
+                    c.start()
+
+        def take(mask):
+            for c in pair(mask, True):
+                c.wait_recv()
 
         def begin():
             for slot in range(3):
                 for axis in range(3):
                     copy(axis, slot).start()
-            pair(0).start()
-
-        def arrive(slots):
-            for slot in slots:
-                for axis in range(3):
-                    copy(axis, slot, True).wait_recv()
-                    part, mask = gather_unit(axis, slot)
-                    got = (part, mask | (1 << axis))
-                    for later in range(3, 7):
-                        for onto in range(3):
-                            if gather_unit(onto, later) == got:
-                                copy(onto, later).start()
-
-        def hooks(i):
+            give(0)
+
+        def arrive(*arrivals):
+            for axis, slot in arrivals:
+                copy(axis, slot, True).wait_recv()
+                part, mask = gather_unit(axis, slot)
+                got = (part, mask | (1 << axis))
+                for later in (3, 4, 5, 6):
+                    for onto in range(3):
+                        if gather_unit(onto, later) == got and not (onto == 1 and later == 4):
+                            copy(onto, later).start()
+                if slot == 1 and axis == gather_unit_source():
+                    copy(1, 4).start()
+
+        def gather_unit_source():
+            return next(a for a in range(3) if gather_unit(1, 5) == (gather_unit(a, 1)[0], 1 << a))
+
+        def hooks(p):
+            @pl.when(p == 0)
+            def _():
+                take(0)
+
+            @pl.when(p == 1)
+            def _():
+                arrive(*((axis, slot) for slot in range(3) for axis in range(3)))
+                give(1, 2, 4)
+
+            @pl.when(p == 2)
+            def _():
+                take(1)
+
+            @pl.when(p == 3)
+            def _():
+                take(2)
+                take(4)
+
+            @pl.when(p == 4)
+            def _():
+                arrive((0, 3), (1, 3), (2, 3), (1, 5), (0, 4))
+                give(3)
+                take(3)
+
+            @pl.when(p == 5)
+            def _():
+                arrive((2, 4), (1, 4), (0, 5), (2, 5))
+                give(5, 6)
+
+            @pl.when(p == 6)
+            def _():
+                take(5)
+                take(6)
+
+        def tail(i):
+            @pl.when(i == 0)
+            def _():
+                for part in range(3):
+                    arrive(((part + 2) % 3, 6))
+                    pair_piece(7, part).start()
+
             @pl.when(i == 1)
             def _():
-                pair(0, True).wait_recv()
-
-            @pl.when(i == 2)
-            def _():
-                arrive((0, 1, 2))
-                for mask in (1, 2, 4):
-                    pair(mask).start()
-
-            @pl.when(i == 8)
-            def _():
-                arrive((3, 4, 5))
-                for mask in (6, 5, 3):
-                    pair(mask).start()
-
-            @pl.when(i == 14)
-            def _():
-                arrive((6,))
-                pair(7).start()
-
-            for step in (5, 6, 7, 11, 12, 13, 15):
-                @pl.when(i == step)
-                def _():
-                    pair(step_order(step)[0], True).wait_recv()
+                take(7)
 
         def drain():
             for axis in range(3):
                 for slot in range(7):
                     copy(axis, slot).wait_send()
             for mask in range(8):
-                pair(mask).wait_send()
-
-        return begin, hooks, drain
-
-    def aggregate(buf, total, hooks, g):
-        @pl.loop(0, NDEV)
-        def _(i):
-            hooks(i)
-            slot = i % RING
-            wait_a(slot)
-            block = block_of(i)
-
-            @pl.loop(0, 2)
-            def _(half):
-                rows = pl.ds(pl.multiple_of(half * 512, 512), 512)
-                if g == 0:
-                    total[0:FROWS, rows] += lax.dot_general(buf[block], abuf[slot, rows, :], NT,
-                                                            preferred_element_type=F32)
-                else:
-                    total[rows, :] += jnp.dot(abuf[slot, rows, :], buf[block], preferred_element_type=F32)
-
+                for c in pair(mask):
+                    c.wait_send()
+
+        return begin, hooks, tail, drain
+
+    def aggregate(buf, total, hooks, tail, g):
+        def product(i):
+            slot = (16 * g + i) % RING
+            if g == 0:
+                return lax.dot_general(buf[block_of(i)], abuf[slot], NT, preferred_element_type=F32)
+            return jnp.dot(abuf[slot], buf[block_of(i)], preferred_element_type=F32)
+
+        def refill(i):
+            slot = (16 * g + i) % RING
             if g == 0:
                 load_a((i + RING) % NDEV, slot).start()
             else:
@@ -202,16 +230,32 @@
                 def _():
                     load_a(i + RING, slot).start()
 
+        rows = pl.ds(0, FROWS if g == 0 else BLK)
+
+        @pl.loop(0, 7)
+        def _(p):
+            hooks(p)
+            wait_a((16 * g + 2 * p) % RING)
+            wait_a((16 * g + 2 * p + 1) % RING)
+            total[rows, :] += product(2 * p) + product(2 * p + 1)
+            refill(2 * p)
+            refill(2 * p + 1)
+
+        @pl.loop(0, 2)
+        def _(k):
+            tail(k)
+            wait_a((16 * g + 14 + k) % RING)
+            total[rows, :] += product(14 + k)
+            refill(14 + k)
+
     def count_copy(d):
         ref = cnt.at[me]
         return remote(ref, ref, ms.at[d], mr.at[d], peer(d))
 
-    begin_x, hooks_x, drain_x = gather(xall, 0)
-    begin_h, hooks_h, drain_h = gather(hall, 1)
+    begin_x, hooks_x, tail_x, drain_x = gather(xall, 0)
+    begin_h, hooks_h, tail_h, drain_h = gather(hall, 1)
 
     begin_x()
-    for d in far_first:
-        count_copy(d).start()
     for load in loads[2:]:
         load.wait()
     w1p[...] = jnp.zeros_like(w1p)
@@ -221,14 +265,16 @@
     w2t[0:NCLS, :] = w2_ref[...].astype(BF16)
     s1acc[...] = jnp.zeros_like(s1acc)
     s2acc[...] = jnp.zeros_like(s2acc)
-    aggregate(xall, s1acc, hooks_x, 0)
+    aggregate(xall, s1acc, hooks_x, tail_x, 0)
 
     s1b[...] = s1acc[...].astype(BF16)
     pre_one = jnp.dot(s1acc[...].T.astype(BF16), w1p[...].astype(BF16), preferred_element_type=F32)
     hall[me] = jnp.maximum(pre_one, 0.0).astype(BF16)
+    begin_h()
+    for d in far_first:
+        count_copy(d).start()
     z1t[...] = jnp.dot(w1t[...], s1b[...], preferred_element_type=F32)
-    begin_h()
-    aggregate(hall, s2acc, hooks_h, 1)
+    aggregate(hall, s2acc, hooks_h, tail_h, 1)
 
     for d in range(1, NDEV):
         ref = cnt.at[peer(d)]
@@ -248,56 +294,39 @@
     gt[...] = grad.astype(BF16)
     ut[...] = lax.dot_general(w2t[...], gt[...], TN, preferred_element_type=F32).astype(BF16)
 
-    def pair_sum(mask):
-        return remote(acc.at[8 + mask], drecv.at[mask], es.at[mask], er.at[mask], dev(0, 1))
-
-    def unit_copy(part, k):
+    def pair_sum(mask, half=None):
+        if half is None:
+            return remote(acc.at[8 + mask], drecv.at[mask], es.at[mask], er.at[mask], dev(0, 1))
+        cols = pl.ds(half * 512, 512)
+        return remote(acc.at[8 + mask, :, cols], drecv.at[mask, :, cols], es.at[mask + half], er.at[mask + half],
+                      dev(0, 1))
+
+    def unit_copy(part, k, half=None):
         axis, mask = reduce_unit(part, k)
         rows = pl.ds(*REDUCE_ROWS[part])
         n = part * 7 + k
-        return remote(acc.at[mask, rows], rbuf.at[k, rows], rs.at[n], rr.at[n], dev(1 << axis))
-
-    def add_rows(mask, source, start, size):
+        if half is None:
+            return remote(acc.at[mask, rows], rbuf.at[k, rows], rs.at[n], rr.at[n], dev(1 << axis))
+        cols = pl.ds(half * 512, 512)
+        n = n if half == 0 else 21 + part
+        return remote(acc.at[mask, rows, cols], rbuf.at[k, rows, cols], rs.at[n], rr.at[n], dev(1 << axis))
+
+    def unit_copies(part, k):
+        return [unit_copy(part, k, half) for half in ((0, 1) if k == 0 else (None,))]
+
+    def add_rows(mask, source, start, size, cols=slice(None)):
         @pl.loop(0, size // 8)
         def _(t):
             rows = pl.ds(pl.multiple_of(start + t * 8, 8), 8)
-            acc[mask, rows, :] += source[rows, :]
+            acc[mask, rows, cols] += source[rows, cols]
 
     def take_pair(mask):
         pair_sum(mask).wait_recv()
         add_rows(mask, drecv.at[mask], 0, HID)
-        for k in range(4):
+        for k in range(1, 4):
             for part in range(3):
                 if reduce_unit(part, k)[1] == mask:
                     unit_copy(part, k).start()
-
-    @pl.loop(0, NDEV)
-    def _(i):
-        slot = (NDEV - 1 - i) % RING
-        mask, other = step_order(NDEV - 1 - i)
-
-        @pl.when(i >= RING)
-        def _():
-            wait_a(slot)
-
-        @pl.loop(0, 2)
-        def _(half):
-            cols = pl.ds(pl.multiple_of(half * 512, 512), 512)
-            acc[mask + 8 * other, :, cols] = jnp.dot(ut[...], abuf[slot, :, cols], preferred_element_type=F32)
-
-        @pl.when(i < NDEV - RING)
-        def _():
-            load_a(NDEV - 1 - i - RING, slot).start()
-
-        for step in range(NDEV):
-            step_mask, step_other = step_order(NDEV - 1 - step)
-
-            @pl.when(i == step)
-            def _():
-                if step_other:
-                    pair_sum(step_mask).start()
-                else:
-                    take_pair(step_mask)
 
     def small_scatter(src, dst, d, base, wait):
         if wait:
@@ -309,42 +338,84 @@
         ref = dst.at[peer(d)] if wait else dst.at[me]
         return remote(ref, ref, ps.at[base + d], pr.at[base + d], peer(d))
 
+    @pl.loop(0, 4)
+    def _(q):
+        other, half = 1 - q // 2, q % 2
+        cols = pl.ds(pl.multiple_of(half * 512, 512), 512)
+        acc[7 + 8 * other, :, cols] = jnp.dot(ut[...], abuf[(30 + other) % RING, :, cols], preferred_element_type=F32)
+        for half in range(2):
+            @pl.when(q == half)
+            def _():
+                pair_sum(7, half).start()
+
+    for j in range(2):
+        load_a(NDEV - 1 - j - RING, (31 - j) % RING).start()
+
     dw2_part = jnp.dot(gt[...], s2b[...], preferred_element_type=F32)
     d2src[...] = jnp.zeros_like(d2src)
     for j in range(6):
-        d2src[j] = dw2_part[j * 8:(j + 1) * 8, 0:128]
-        d2src[6 + j] = dw2_part[j * 8:(j + 1) * 8, 128:256]
-    d2src[12] = jnp.full((8, 128), loss_part, F32)
+        for k in range(2):
+            d2src[6 * k + j] = dw2_part[j * 8:(j + 1) * 8, k * 128:(k + 1) * 128]
+    d2src[12] = jnp.full(TILE, loss_part, F32)
     d2r1[me] = d2src[me]
     for d in far_first:
         small_scatter(d2src, d2r1, d, 0, False).start()
 
+    for half in range(2):
+        pair_sum(7, half).wait_recv()
+        add_rows(7, drecv.at[7], 0, HID, pl.ds(half * 512, 512))
+        for part in range(3):
+            unit_copy(part, 0, half).start()
+
+    @pl.loop(1, 8)
+    def _(p):
+        for k in range(2):
+            @pl.when(p >= 3)
+            def _():
+                wait_a((31 - 2 * p - k) % RING)
+        for k in range(2):
+            mask, other = step_order(NDEV - 1 - 2 * p - k)
+            acc[mask + 8 * other] = jnp.dot(ut[...], abuf[(31 - 2 * p - k) % RING], preferred_element_type=F32)
+        for k in range(2):
+            @pl.when(p < 5)
+            def _():
+                load_a(NDEV - 1 - 2 * p - k - RING, (31 - 2 * p - k) % RING).start()
+
+        for step in range(2, NDEV):
+            step_mask, step_other = step_order(NDEV - 1 - step)
+
+            @pl.when(p == step // 2)
+            def _():
+                if step_other:
+                    pair_sum(step_mask).start()
+                else:
+                    take_pair(step_mask)
+
     def take_unit(part, k, send=None):
         axis, mask = reduce_unit(part, k)
-        unit_copy(part, k).wait_recv()
+        for c in unit_copies(part, k):
+            c.wait_recv()
         add_rows(mask - (1 << axis), rbuf.at[k], *REDUCE_ROWS[part])
         if send is not None:
             unit_copy(part, send).start()
 
-    for part in range(3):
-        take_unit(part, 0, 4)
-    for part in range(3):
-        take_unit(part, 1, 5)
+    for k in range(2):
+        for part in range(3):
+            take_unit(part, k, k + 4)
     for part in range(3):
         take_unit(part, 2)
     for d in range(1, NDEV):
         small_scatter(d2src, d2r1, d, 0, True).wait_recv()
     d2r2[me] = jnp.sum(d2r1[...], axis=0)
-    for d in far_first:
-        small_gather(d2r2, d, 16, False).start()
     for part in range(3):
         take_unit(part, 3)
     for part in range(3):
         take_unit(part, 4, 6)
-    for part in range(3):
-        take_unit(part, 5)
-    for part in range(3):
-        take_unit(part, 6)
+    for d in far_first:
+        small_gather(d2r2, d, 16, False).start()
+    for k in (5, 6):
+        for part in range(3):
+            take_unit(part, k)
 
     grad_one = jnp.where(z1t[...] > 0.0, acc[0], 0.0).astype(BF16)
     d1src[...] = lax.dot_general(grad_one, s1b[...], NT, preferred_element_type=F32).reshape(NDEV, 16, FPAD)
@@ -353,9 +424,8 @@
         small_scatter(d1src, d1r1, d, 32, False).start()
     for d in range(1, NDEV):
         small_gather(d2r2, d, 16, True).wait_recv()
-    left = d2r2[0:6].reshape(CPAD, 128)
-    right = d2r2[6:12].reshape(CPAD, 128)
-    dw2_ref[...] = jnp.concatenate([left, right], axis=1)
+    for k in range(2):
+        dw2_ref[:, pl.ds(k * 128, 128)] = d2r2[pl.ds(6 * k, 6)].reshape(CPAD, 128)
     loss_ref[...] = d2r2[12] / label_count
     for d in range(1, NDEV):
         small_scatter(d1src, d1r1, d, 32, True).wait_recv()
@@ -364,11 +434,14 @@
         small_gather(d1r2, d, 48, False).start()
     drain_x()
     drain_h()
-    for mask in range(8):
+    for mask in range(7):
         pair_sum(mask).wait_send()
+    for half in range(2):
+        pair_sum(7, half).wait_send()
     for part in range(3):
         for k in range(7):
-            unit_copy(part, k).wait_send()
+            for c in unit_copies(part, k):
+                c.wait_send()
     for d in range(1, NDEV):
         count_copy(d).wait_send()
         small_scatter(d2src, d2r1, d, 0, False).wait_send()
@@ -394,7 +467,7 @@
         dma = pltpu.SemaphoreType.DMA
         parts = pl.pallas_call(
             kernel,
-            out_shape=(jax.ShapeDtypeStruct((8, 128), F32), jax.ShapeDtypeStruct((HID, FPAD), F32),
+            out_shape=(jax.ShapeDtypeStruct(TILE, F32), jax.ShapeDtypeStruct((HID, FPAD), F32),
                        jax.ShapeDtypeStruct((CPAD, HID), F32)),
             in_specs=[hbm] * 6,
             out_specs=(vmem, vmem, vmem),
@@ -420,18 +493,13 @@
                 pltpu.VMEM((8, HID, BLK), F32),
                 pltpu.VMEM((7, HID, BLK), F32),
                 pltpu.VMEM((CPAD, BLK), BF16),
-                pltpu.VMEM((NDEV, 8, 128), F32),
-                pltpu.VMEM((NDEV, 8, 128), F32),
-                pltpu.VMEM((NDEV, 8, 128), F32),
-                pltpu.VMEM((NDEV, 8, 128), F32),
-                pltpu.VMEM((NDEV, 16, FPAD), F32),
-                pltpu.VMEM((NDEV, 16, FPAD), F32),
-                pltpu.VMEM((NDEV, 16, FPAD), F32),
-                dma((RING,)), dma((5,)), dma((42,)), dma((42,)), dma((16,)), dma((16,)), dma((21,)), dma((21,)),
-                dma((8,)), dma((8,)), dma((16,)), dma((16,)), dma((64,)), dma((64,)),
+                pltpu.VMEM((NDEV, 1, 128), F32),
+                *[pltpu.VMEM((NDEV, *TILE), F32)] * 3,
+                *[pltpu.VMEM((NDEV, 16, FPAD), F32)] * 3,
+                *[dma((SEMS,))] * 14,
             ],
             compiler_params=pltpu.CompilerParams(collective_id=0, has_side_effects=True,
-                                                 vmem_limit_bytes=62 * 1000 * 1000),
+                                                 vmem_limit_bytes=67 * 1000 * 1000),
         )(adj_rows, feat_rows.T, w_one, w_two.T, label_rows.reshape(1, BLK), mask_rows.reshape(1, BLK))
         loss, dw_one, dw_two = pl.pallas_call(
             finish,

time: 138 us -> 135 us (0.978)
  Pallas kernels: 137 us -> 135 us
    pallas_call x1, Pallas kernels: 136 us -> 133 us  [local_step(): pl.pallas_call(kernel, out_shape=(jax.ShapeDtypeStruct(TILE, F32), jax.Sh...]
where the time goes in v3:
time: 135 us
  Pallas kernels  135 us (100%)
    pallas_call x1, Pallas kernels, local_step(): pl.pallas_call(kernel, out_shape=(jax.ShapeDtypeStruct(TILE, F32), jax.Sh...  133 us

profile of v3, /device:TPU:0, one launch (start us, length us, event | category | flops | bytes accessed | tf_op | source)
XLA Modules:
  0.0 135.2 jit_solution(17248998352692464634)
XLA Ops:
  0.6 132.9 %shard_map.85 = (f32[8,128]{1,0:T(8,128)}, f32[256,128]{1,0:T(8,128)}, f32[48,256]{1,0:T(8,128)}) custom-call(bf16[1024,16384]{1,0:T(8,128)(2,1)} %a_hbm.1, bf16[100,1024]{1,0:T(8,128)(2,1)} %bitcast.6, f32[100,256]{1,0:T(8,128)} %w1_hbm.1, f32[47,256]{1,0:T(8,128)} %bitcast.7, s32[1,1024]{1,0:T(1,128)} %bitcast.8, s32[1,1024]{1,0:T(1,128)} %bitcast.9), custom_call_target="tpu_custom_call" | custom-call | tf_op jit(solution)/shard_map/pallas_call | solution.py:468
  133.5 1.7 %shard_map.86 = (f32[1,1]{1,0:T(1,128)}, f32[100,256]{1,0:T(8,128)}, f32[47,256]{1,0:T(8,128)}) custom-call(f32[8,128]{1,0:T(8,128)} %get-tuple-element.9.loss_ref, f32[256,128]{1,0:T(8,128)} %get-tuple-element.10.dw1_ref, f32[48,256]{1,0:T(8,128)} %get-tuple-element.11.dw2_ref), custom_call_target="tpu_custom_call" | custom-call | tf_op jit(solution)/shard_map/pallas_call | solution.py:504

commit v4 on v3

--- a/solution.py
+++ b/solution.py
@@ -16,7 +16,6 @@
 HID = 256
 NCLS, CPAD = 47, 48
 RING = 6
-SEMS = 64
 TILE = (8, 128)
 
 ORDER = tuple((p, (p + 1) % 3, (p + 2) % 3) for p in range(3))
@@ -61,11 +60,11 @@
     return bit + by - 2 * bit * by
 
 
-def kernel(a_hbm, x_hbm, w1_hbm, w2_hbm, y_hbm, m_hbm, loss_ref, dw1_ref, dw2_ref,
+def kernel(a_hbm, x_hbm, w1_hbm, w2_hbm, y_hbm, m_hbm, d1out, d2out,
            abuf, xin, w1_ref, w2_ref, y_ref, m_ref, xall, hall, s1acc, s2acc, s1b, s2b, z1t, w1p, w1t, w2t, ut,
            acc, drecv, rbuf, gt,
            cnt, d2src, d2r1, d2r2, d1src, d1r1, d1r2,
-           asem, xsem, gs, gr, ds, dr, rs, rr, es, er, ms, mr, ps, pr):
+           asem, xsem, gr, dr, rr, er, pr, snd):
     me = lax.axis_index(AXIS)
     core, px, py, pz = me % 2, (me // 2) % 2, (me // 4) % 2, me // 8
 
@@ -118,7 +117,7 @@
             owner = dev(mask | (1 << axis) if at_receiver else mask)
             ref = piece(owner, part)
             n = g * 21 + axis * 7 + slot
-            return remote(ref, ref, gs.at[n], gr.at[n], dev(1 << axis))
+            return remote(ref, ref, snd.at[g], gr.at[n], dev(1 << axis))
 
         def pair(mask, at_receiver=False):
             return [pair_piece(mask, k, at_receiver) for k in range(1 if mask < 7 else 3)]
@@ -126,7 +125,7 @@
         def pair_piece(mask, k, at_receiver=False):
             owner = dev(mask, 1 if at_receiver else 0)
             ref = buf.at[owner] if mask < 7 else piece(owner, k)
-            return remote(ref, ref, ds.at[g * 10 + mask + k], dr.at[g * 10 + mask + k], dev(0, 1))
+            return remote(ref, ref, snd.at[g], dr.at[g * 10 + mask + k], dev(0, 1))
 
         def give(*masks):
             for mask in masks:
@@ -205,12 +204,8 @@
                 take(7)
 
         def drain():
-            for axis in range(3):
-                for slot in range(7):
-                    copy(axis, slot).wait_send()
-            for mask in range(8):
-                for c in pair(mask):
-                    c.wait_send()
+            every = buf.at[pl.ds(0, 15)]
+            remote(every, every, snd.at[g], gr.at[0], me).wait_send()
 
         return begin, hooks, tail, drain
 
@@ -248,9 +243,13 @@
             total[rows, :] += product(14 + k)
             refill(14 + k)
 
-    def count_copy(d):
-        ref = cnt.at[me]
-        return remote(ref, ref, ms.at[d], mr.at[d], peer(d))
+    def small(x, src, dst, scatter=False):
+        for d in far_first:
+            remote(src.at[peer(d)] if scatter else src, dst.at[me], snd.at[3 + x], pr.at[x], peer(d)).start()
+
+    def small_wait(x, dst):
+        ref = dst.at[pl.ds(0, 15)]
+        remote(ref, ref, snd.at[3 + x], pr.at[x], me).wait()
 
     begin_x, hooks_x, tail_x, drain_x = gather(xall, 0)
     begin_h, hooks_h, tail_h, drain_h = gather(hall, 1)
@@ -271,14 +270,11 @@
     pre_one = jnp.dot(s1acc[...].T.astype(BF16), w1p[...].astype(BF16), preferred_element_type=F32)
     hall[me] = jnp.maximum(pre_one, 0.0).astype(BF16)
     begin_h()
-    for d in far_first:
-        count_copy(d).start()
+    small(0, cnt.at[me], cnt)
     z1t[...] = jnp.dot(w1t[...], s1b[...], preferred_element_type=F32)
     aggregate(hall, s2acc, hooks_h, tail_h, 1)
 
-    for d in range(1, NDEV):
-        ref = cnt.at[peer(d)]
-        remote(ref, ref, ms.at[d], mr.at[d], peer(d)).wait_recv()
+    small_wait(0, cnt)
     label_count = jnp.sum(cnt[...], axis=0)[0:1, 0:1]
     s2b[...] = s2acc[...].astype(BF16)
     logits = lax.dot_general(w2t[...], s2b[...], NT, preferred_element_type=F32)
@@ -296,9 +292,9 @@
 
     def pair_sum(mask, half=None):
         if half is None:
-            return remote(acc.at[8 + mask], drecv.at[mask], es.at[mask], er.at[mask], dev(0, 1))
+            return remote(acc.at[8 + mask], drecv.at[mask], snd.at[2], er.at[mask], dev(0, 1))
         cols = pl.ds(half * 512, 512)
-        return remote(acc.at[8 + mask, :, cols], drecv.at[mask, :, cols], es.at[mask + half], er.at[mask + half],
+        return remote(acc.at[8 + mask, :, cols], drecv.at[mask, :, cols], snd.at[2], er.at[mask + half],
                       dev(0, 1))
 
     def unit_copy(part, k, half=None):
@@ -306,10 +302,10 @@
         rows = pl.ds(*REDUCE_ROWS[part])
         n = part * 7 + k
         if half is None:
-            return remote(acc.at[mask, rows], rbuf.at[k, rows], rs.at[n], rr.at[n], dev(1 << axis))
+            return remote(acc.at[mask, rows], rbuf.at[k, rows], snd.at[2], rr.at[n], dev(1 << axis))
         cols = pl.ds(half * 512, 512)
         n = n if half == 0 else 21 + part
-        return remote(acc.at[mask, rows, cols], rbuf.at[k, rows, cols], rs.at[n], rr.at[n], dev(1 << axis))
+        return remote(acc.at[mask, rows, cols], rbuf.at[k, rows, cols], snd.at[2], rr.at[n], dev(1 << axis))
 
     def unit_copies(part, k):
         return [unit_copy(part, k, half) for half in ((0, 1) if k == 0 else (None,))]
@@ -328,16 +324,6 @@
                 if reduce_unit(part, k)[1] == mask:
                     unit_copy(part, k).start()
 
-    def small_scatter(src, dst, d, base, wait):
-        if wait:
-            ref = dst.at[peer(d)]
-            return remote(ref, ref, ps.at[base + d], pr.at[base + d], peer(d))
-        return remote(src.at[peer(d)], dst.at[me], ps.at[base + d], pr.at[base + d], peer(d))
-
-    def small_gather(dst, d, base, wait):
-        ref = dst.at[peer(d)] if wait else dst.at[me]
-        return remote(ref, ref, ps.at[base + d], pr.at[base + d], peer(d))
-
     @pl.loop(0, 4)
     def _(q):
         other, half = 1 - q // 2, q % 2
@@ -357,9 +343,10 @@
         for k in range(2):
             d2src[6 * k + j] = dw2_part[j * 8:(j + 1) * 8, k * 128:(k + 1) * 128]
     d2src[12] = jnp.full(TILE, loss_part, F32)
+    d2src[13] = jnp.full(TILE, jnp.sum(weight), F32)
+    keep_two = pltpu.make_async_copy(d2r2, d2out.at[me], xsem.at[0])
     d2r1[me] = d2src[me]
-    for d in far_first:
-        small_scatter(d2src, d2r1, d, 0, False).start()
+    small(1, d2src, d2r1, True)
 
     for half in range(2):
         pair_sum(7, half).wait_recv()
@@ -404,15 +391,14 @@
             take_unit(part, k, k + 4)
     for part in range(3):
         take_unit(part, 2)
-    for d in range(1, NDEV):
-        small_scatter(d2src, d2r1, d, 0, True).wait_recv()
-    d2r2[me] = jnp.sum(d2r1[...], axis=0)
+    small_wait(1, d2r1)
+    d2r2[...] = jnp.sum(d2r1[...], axis=0)
     for part in range(3):
         take_unit(part, 3)
     for part in range(3):
         take_unit(part, 4, 6)
-    for d in far_first:
-        small_gather(d2r2, d, 16, False).start()
+    small(2, d2r2, d2out)
+    keep_two.start()
     for k in (5, 6):
         for part in range(3):
             take_unit(part, k)
@@ -420,44 +406,26 @@
     grad_one = jnp.where(z1t[...] > 0.0, acc[0], 0.0).astype(BF16)
     d1src[...] = lax.dot_general(grad_one, s1b[...], NT, preferred_element_type=F32).reshape(NDEV, 16, FPAD)
     d1r1[me] = d1src[me]
-    for d in far_first:
-        small_scatter(d1src, d1r1, d, 32, False).start()
-    for d in range(1, NDEV):
-        small_gather(d2r2, d, 16, True).wait_recv()
-    for k in range(2):
-        dw2_ref[:, pl.ds(k * 128, 128)] = d2r2[pl.ds(6 * k, 6)].reshape(CPAD, 128)
-    loss_ref[...] = d2r2[12] / label_count
-    for d in range(1, NDEV):
-        small_scatter(d1src, d1r1, d, 32, True).wait_recv()
-    d1r2[me] = jnp.sum(d1r1[...], axis=0)
-    for d in far_first:
-        small_gather(d1r2, d, 48, False).start()
+    small(3, d1src, d1r1, True)
     drain_x()
     drain_h()
-    for mask in range(7):
-        pair_sum(mask).wait_send()
-    for half in range(2):
-        pair_sum(7, half).wait_send()
-    for part in range(3):
-        for k in range(7):
-            for c in unit_copies(part, k):
-                c.wait_send()
-    for d in range(1, NDEV):
-        count_copy(d).wait_send()
-        small_scatter(d2src, d2r1, d, 0, False).wait_send()
-        small_gather(d2r2, d, 16, False).wait_send()
-        small_scatter(d1src, d1r1, d, 32, False).wait_send()
-    for d in range(1, NDEV):
-        small_gather(d1r2, d, 48, True).wait_recv()
-    dw1_ref[...] = d1r2[...].reshape(HID, FPAD)
-    for d in range(1, NDEV):
-        small_gather(d1r2, d, 48, False).wait_send()
-
-
-def finish(loss_ref, dw1_ref, dw2_ref, loss_out, dw1_out, dw2_out):
-    loss_out[...] = loss_ref[0:1, 0:1]
-    dw1_out[...] = dw1_ref[...].T[0:FIN, :]
-    dw2_out[...] = dw2_ref[0:NCLS, :]
+    remote(acc.at[pl.ds(0, 15)], acc.at[pl.ds(0, 15)], snd.at[2], pr.at[0], me).wait_send()
+    small_wait(2, d2out)
+    keep_two.wait()
+    small_wait(3, d1r1)
+    d1r2[...] = jnp.sum(d1r1[...], axis=0)
+    small(4, d1r2, d1out)
+    keep_one = pltpu.make_async_copy(d1r2, d1out.at[me], xsem.at[1])
+    keep_one.start()
+    keep_one.wait()
+    small_wait(4, d1out)
+
+
+def finish(d1_ref, d2_ref, loss_out, dw1_out, dw2_out):
+    loss_out[...] = d2_ref[12, 0:1, 0:1] / d2_ref[13, 0:1, 0:1]
+    dw1_out[...] = d1_ref[...].reshape(HID, FPAD).T[0:FIN, :]
+    for k in range(2):
+        dw2_out[:, pl.ds(k * 128, 128)] = d2_ref[pl.ds(6 * k, 6)].reshape(CPAD, 128)[0:NCLS]
 
 
 def solution(mesh):
@@ -467,10 +435,9 @@
         dma = pltpu.SemaphoreType.DMA
         parts = pl.pallas_call(
             kernel,
-            out_shape=(jax.ShapeDtypeStruct(TILE, F32), jax.ShapeDtypeStruct((HID, FPAD), F32),
-                       jax.ShapeDtypeStruct((CPAD, HID), F32)),
+            out_shape=(jax.ShapeDtypeStruct((NDEV, 16, FPAD), F32), jax.ShapeDtypeStruct((NDEV, *TILE), F32)),
             in_specs=[hbm] * 6,
-            out_specs=(vmem, vmem, vmem),
+            out_specs=(hbm, hbm),
             scratch_shapes=[
                 pltpu.VMEM((RING, BLK, BLK), BF16),
                 pltpu.VMEM((FIN, BLK), BF16),
@@ -494,9 +461,11 @@
                 pltpu.VMEM((7, HID, BLK), F32),
                 pltpu.VMEM((CPAD, BLK), BF16),
                 pltpu.VMEM((NDEV, 1, 128), F32),
-                *[pltpu.VMEM((NDEV, *TILE), F32)] * 3,
-                *[pltpu.VMEM((NDEV, 16, FPAD), F32)] * 3,
-                *[dma((SEMS,))] * 14,
+                *[pltpu.VMEM((NDEV, *TILE), F32)] * 2,
+                pltpu.VMEM(TILE, F32),
+                *[pltpu.VMEM((NDEV, 16, FPAD), F32)] * 2,
+                pltpu.VMEM((16, FPAD), F32),
+                *[dma((n,)) for n in (RING, 5, 42, 20, 24, 9, 5, 8)],
             ],
             compiler_params=pltpu.CompilerParams(collective_id=0, has_side_effects=True,
                                                  vmem_limit_bytes=67 * 1000 * 1000),
@@ -505,7 +474,7 @@
             finish,
             out_shape=(jax.ShapeDtypeStruct((1, 1), F32), jax.ShapeDtypeStruct((FIN, HID), F32),
                        jax.ShapeDtypeStruct((NCLS, HID), F32)),
-            in_specs=[vmem] * 3,
+            in_specs=[vmem] * 2,
             out_specs=(vmem, vmem, vmem),
         )(*parts)
         return loss.reshape(1), dw_one, dw_two.T

time: 135 us -> 128 us (0.948)
  Pallas kernels: 135 us -> 127 us
    pallas_call x1, Pallas kernels: 133 us -> 125 us  [local_step(): pl.pallas_call(kernel, out_shape=(jax.ShapeDtypeStruct((NDEV, 16, FPAD),...]
where the time goes in v4:
time: 128 us; the launch traced here: 127 us
  Pallas kernels  127 us (99%)
    pallas_call x1, Pallas kernels, local_step(): pl.pallas_call(kernel, out_shape=(jax.ShapeDtypeStruct((NDEV, 16, FPAD),...  125 us

profile of v4, /device:TPU:0, one launch (start us, length us, event | category | flops | bytes accessed | tf_op | source)
XLA Modules:
  0.0 127.5 jit_solution(4853418426711185483)
XLA Ops:
  0.6 125.2 %shard_map.85 = (f32[16,16,128]{2,1,0:T(8,128)}, f32[16,8,128]{2,1,0:T(8,128)}) custom-call(bf16[1024,16384]{1,0:T(8,128)(2,1)} %a_hbm.1, bf16[100,1024]{1,0:T(8,128)(2,1)} %bitcast.6, f32[100,256]{1,0:T(8,128)} %w1_hbm.1, f32[47,256]{1,0:T(8,128)} %bitcast.7, s32[1,1024]{1,0:T(1,128)} %bitcast.8, s32[1,1024]{1,0:T(1,128)} %bitcast.9), custom_call_target="tpu_custom_call" | custom-call | tf_op jit(solution)/shard_map/pallas_call | solution.py:436
  125.8 1.7 %shard_map.86 = (f32[1,1]{1,0:T(1,128)}, f32[100,256]{1,0:T(8,128)}, f32[47,256]{1,0:T(8,128)}) custom-call(f32[16,16,128]{2,1,0:T(8,128)} %get-tuple-element.8.d1_ref, f32[16,8,128]{2,1,0:T(8,128)} %get-tuple-element.9.d2_ref), custom_call_target="tpu_custom_call" | custom-call | tf_op jit(solution)/shard_map/pallas_call | solution.py:473

commit v5 on v4

--- a/solution.py
+++ b/solution.py
@@ -92,15 +92,15 @@
 
     far_first = sorted(range(1, NDEV), key=lambda d: -bin(d // 2).count('1'))
 
+    barrier = pltpu.get_barrier_semaphore()
+    for d in (8, 4, 2, 1):
+        pl.semaphore_signal(barrier, inc=1, device_id=(peer(d),), device_id_type=MESH)
     loads = [pltpu.make_async_copy(src, dst, xsem.at[k]) for k, (src, dst) in enumerate((
         (x_hbm, xin), (m_hbm, m_ref), (w1_hbm, w1_ref), (w2_hbm, w2_ref), (y_hbm, y_ref)))]
     for load in loads:
         load.start()
     for i in range(RING):
         load_a(i, i).start()
-    barrier = pltpu.get_barrier_semaphore()
-    for d in (8, 4, 2, 1):
-        pl.semaphore_signal(barrier, inc=1, device_id=(peer(d),), device_id_type=MESH)
     xall[me] = jnp.zeros((FROWS, BLK), BF16)
     loads[0].wait()
     xall[me, 0:FIN, :] = xin[...]
@@ -112,29 +112,24 @@
         def piece(owner, part):
             return buf.at[owner, :, pl.ds(*GATHER_COLS[part])] if g == 0 else buf.at[owner, pl.ds(*GATHER_ROWS[part])]
 
-        def copy(axis, slot, at_receiver=False):
+        def copy(axis, slot):
             part, mask = gather_unit(axis, slot)
-            owner = dev(mask | (1 << axis) if at_receiver else mask)
-            ref = piece(owner, part)
-            n = g * 21 + axis * 7 + slot
+            ref = piece(dev(mask), part)
+            n = g * 11 + (slot if slot < 4 else 4 if slot == 6 else 2 * axis + slot + 1)
             return remote(ref, ref, snd.at[g], gr.at[n], dev(1 << axis))
 
-        def pair(mask, at_receiver=False):
-            return [pair_piece(mask, k, at_receiver) for k in range(1 if mask < 7 else 3)]
-
-        def pair_piece(mask, k, at_receiver=False):
-            owner = dev(mask, 1 if at_receiver else 0)
-            ref = buf.at[owner] if mask < 7 else piece(owner, k)
-            return remote(ref, ref, snd.at[g], dr.at[g * 10 + mask + k], dev(0, 1))
+        def whole(sems, n):
+            return remote(buf.at[me], buf.at[me], snd.at[g], sems.at[n], me)
 
         def give(*masks):
             for mask in masks:
-                for c in pair(mask):
-                    c.start()
-
-        def take(mask):
-            for c in pair(mask, True):
-                c.wait_recv()
+                owner = dev(mask)
+                for ref in [buf.at[owner]] if mask < 7 else [piece(owner, part) for part in range(3)]:
+                    remote(ref, ref, snd.at[g], dr.at[g * 8 + mask], dev(0, 1)).start()
+
+        def take(*masks):
+            for mask in masks:
+                whole(dr, g * 8 + mask).wait_recv()
 
         def begin():
             for slot in range(3):
@@ -142,20 +137,20 @@
                     copy(axis, slot).start()
             give(0)
 
-        def arrive(*arrivals):
-            for axis, slot in arrivals:
-                copy(axis, slot, True).wait_recv()
-                part, mask = gather_unit(axis, slot)
-                got = (part, mask | (1 << axis))
-                for later in (3, 4, 5, 6):
-                    for onto in range(3):
-                        if gather_unit(onto, later) == got and not (onto == 1 and later == 4):
-                            copy(onto, later).start()
-                if slot == 1 and axis == gather_unit_source():
-                    copy(1, 4).start()
-
-        def gather_unit_source():
-            return next(a for a in range(3) if gather_unit(1, 5) == (gather_unit(a, 1)[0], 1 << a))
+        def forward(axis, slot, *onto):
+            part, mask = gather_unit(axis, slot)
+            for over, later in onto:
+                assert gather_unit(over, later) == (part, mask | (1 << axis))
+                copy(over, later).start()
+
+        def arrive(*slots):
+            for slot in slots:
+                whole(gr, g * 11 + min(slot, 4)).wait_recv()
+
+        def arrive_one(axis, slot):
+            part, mask = gather_unit(axis, slot)
+            ref = piece(dev(mask | (1 << axis)), part)
+            remote(ref, ref, snd.at[g], gr.at[g * 11 + 2 * axis + slot + 1], me).wait_recv()
 
         def hooks(p):
             @pl.when(p == 0)
@@ -164,7 +159,15 @@
 
             @pl.when(p == 1)
             def _():
-                arrive(*((axis, slot) for slot in range(3) for axis in range(3)))
+                for slot in range(3):
+                    arrive(slot)
+                    for over in range(3):
+                        if slot == 0:
+                            forward((over + 2) % 3, 0, (over, 3))
+                        if slot == 1:
+                            forward((over + 2) % 3, 1, (over, 5))
+                        if (slot == 0) == (over != 1) and slot < 2:
+                            forward((over + 1) % 3, 0, (over, 4))
                 give(1, 2, 4)
 
             @pl.when(p == 2)
@@ -173,31 +176,35 @@
 
             @pl.when(p == 3)
             def _():
-                take(2)
-                take(4)
+                take(2, 4)
 
             @pl.when(p == 4)
             def _():
-                arrive((0, 3), (1, 3), (2, 3), (1, 5), (0, 4))
+                arrive(3)
+                for over in range(3):
+                    forward((over + 2) % 3, 3, (over, 6))
+                arrive_one(1, 5)
+                arrive_one(0, 4)
                 give(3)
                 take(3)
 
             @pl.when(p == 5)
             def _():
-                arrive((2, 4), (1, 4), (0, 5), (2, 5))
+                arrive_one(2, 4)
+                arrive_one(1, 4)
+                arrive_one(0, 5)
+                arrive_one(2, 5)
                 give(5, 6)
 
             @pl.when(p == 6)
             def _():
-                take(5)
-                take(6)
+                take(5, 6)
 
         def tail(i):
             @pl.when(i == 0)
             def _():
-                for part in range(3):
-                    arrive(((part + 2) % 3, 6))
-                    pair_piece(7, part).start()
+                arrive(6)
+                give(7)
 
             @pl.when(i == 1)
             def _():
@@ -205,7 +212,7 @@
 
         def drain():
             every = buf.at[pl.ds(0, 15)]
-            remote(every, every, snd.at[g], gr.at[0], me).wait_send()
+            remote(every, every, snd.at[g], gr.at[g], me).wait_send()
 
         return begin, hooks, tail, drain
 
@@ -300,15 +307,10 @@
     def unit_copy(part, k, half=None):
         axis, mask = reduce_unit(part, k)
         rows = pl.ds(*REDUCE_ROWS[part])
-        n = part * 7 + k
         if half is None:
-            return remote(acc.at[mask, rows], rbuf.at[k, rows], snd.at[2], rr.at[n], dev(1 << axis))
+            return remote(acc.at[mask, rows], rbuf.at[k, rows], snd.at[2], rr.at[k], dev(1 << axis))
         cols = pl.ds(half * 512, 512)
-        n = n if half == 0 else 21 + part
-        return remote(acc.at[mask, rows, cols], rbuf.at[k, rows, cols], snd.at[2], rr.at[n], dev(1 << axis))
-
-    def unit_copies(part, k):
-        return [unit_copy(part, k, half) for half in ((0, 1) if k == 0 else (None,))]
+        return remote(acc.at[mask, rows, cols], rbuf.at[k, rows, cols], snd.at[2], rr.at[k], dev(1 << axis))
 
     def add_rows(mask, source, start, size, cols=slice(None)):
         @pl.loop(0, size // 8)
@@ -378,32 +380,29 @@
                 else:
                     take_pair(step_mask)
 
-    def take_unit(part, k, send=None):
-        axis, mask = reduce_unit(part, k)
-        for c in unit_copies(part, k):
-            c.wait_recv()
-        add_rows(mask - (1 << axis), rbuf.at[k], *REDUCE_ROWS[part])
-        if send is not None:
-            unit_copy(part, send).start()
-
-    for k in range(2):
+    def units_wait(k):
+        remote(rbuf.at[k], rbuf.at[k], snd.at[2], rr.at[k], me).wait_recv()
+
+    def take_units(k, send=None):
+        units_wait(k)
         for part in range(3):
-            take_unit(part, k, k + 4)
-    for part in range(3):
-        take_unit(part, 2)
+            axis, mask = reduce_unit(part, k)
+            add_rows(mask - (1 << axis), rbuf.at[k], *REDUCE_ROWS[part])
+            if send is not None:
+                unit_copy(part, send).start()
+
+    take_units(0, 4)
+    take_units(1, 5)
+    take_units(2)
     small_wait(1, d2r1)
     d2r2[...] = jnp.sum(d2r1[...], axis=0)
-    for part in range(3):
-        take_unit(part, 3)
-    for part in range(3):
-        take_unit(part, 4, 6)
+    take_units(3)
+    take_units(4, 6)
     small(2, d2r2, d2out)
     keep_two.start()
-    for k in (5, 6):
-        for part in range(3):
-            take_unit(part, k)
-
-    grad_one = jnp.where(z1t[...] > 0.0, acc[0], 0.0).astype(BF16)
+    take_units(5)
+    units_wait(6)
+    grad_one = jnp.where(z1t[...] > 0.0, acc[0] + rbuf[6], 0.0).astype(BF16)
     d1src[...] = lax.dot_general(grad_one, s1b[...], NT, preferred_element_type=F32).reshape(NDEV, 16, FPAD)
     d1r1[me] = d1src[me]
     small(3, d1src, d1r1, True)
@@ -465,7 +464,7 @@
                 pltpu.VMEM(TILE, F32),
                 *[pltpu.VMEM((NDEV, 16, FPAD), F32)] * 2,
                 pltpu.VMEM((16, FPAD), F32),
-                *[dma((n,)) for n in (RING, 5, 42, 20, 24, 9, 5, 8)],
+                *[dma((n,)) for n in (RING, 5, 22, 16, 7, 9, 5, 8)],
             ],
             compiler_params=pltpu.CompilerParams(collective_id=0, has_side_effects=True,
                                                  vmem_limit_bytes=67 * 1000 * 1000),

time: 128 us -> 127 us (level)
  no operation moved by 1% of the time
where the time goes in v5:
time: 127 us
  Pallas kernels  126 us (99%)
    pallas_call x1, Pallas kernels, local_step(): pl.pallas_call(kernel, out_shape=(jax.ShapeDtypeStruct((NDEV, 16, FPAD),...  125 us

profile of v5, /device:TPU:0, one launch (start us, length us, event | category | flops | bytes accessed | tf_op | source)
XLA Modules:
  0.0 127.0 jit_solution(16895214168065824372)
XLA Ops:
  0.6 124.7 %shard_map.85 = (f32[16,16,128]{2,1,0:T(8,128)}, f32[16,8,128]{2,1,0:T(8,128)}) custom-call(bf16[1024,16384]{1,0:T(8,128)(2,1)} %a_hbm.1, bf16[100,1024]{1,0:T(8,128)(2,1)} %bitcast.6, f32[100,256]{1,0:T(8,128)} %w1_hbm.1, f32[47,256]{1,0:T(8,128)} %bitcast.7, s32[1,1024]{1,0:T(1,128)} %bitcast.8, s32[1,1024]{1,0:T(1,128)} %bitcast.9), custom_call_target="tpu_custom_call" | custom-call | tf_op jit(solution)/shard_map/pallas_call | solution.py:435
  125.3 1.7 %shard_map.86 = (f32[1,1]{1,0:T(1,128)}, f32[100,256]{1,0:T(8,128)}, f32[47,256]{1,0:T(8,128)}) custom-call(f32[16,16,128]{2,1,0:T(8,128)} %get-tuple-element.8.d1_ref, f32[16,8,128]{2,1,0:T(8,128)} %get-tuple-element.9.d2_ref), custom_call_target="tpu_custom_call" | custom-call | tf_op jit(solution)/shard_map/pallas_call | solution.py:472

commit v6 on v5

--- a/solution.py
+++ b/solution.py
@@ -18,7 +18,10 @@
 RING = 6
 TILE = (8, 128)
 
-ORDER = tuple((p, (p + 1) % 3, (p + 2) % 3) for p in range(3))
+AXES, BOTH = range(3), range(2)
+BIT = (1, 2, 4)
+SOURCE = (0, 0, 0, 1, 1, 2, 4)
+ORDER = tuple((p, (p + 1) % 3, (p + 2) % 3) for p in AXES)
 GATHER_ROWS = ((0, 352), (352, 336), (688, 336))
 GATHER_COLS = ((0, 384), (384, 384), (768, 256))
 REDUCE_ROWS = ((0, 88), (88, 88), (176, 80))
@@ -43,7 +46,7 @@
 
 def reduce_unit(part, k):
     b1, b2, b3 = ORDER[part]
-    m1, m2, m3 = 1 << b1, 1 << b2, 1 << b3
+    m1, m2, m3 = BIT[b1], BIT[b2], BIT[b3]
     return ((b1, m1 | m2 | m3), (b1, m1 | m2), (b1, m1 | m3), (b1, m1), (b2, m2 | m3), (b2, m2), (b3, m3))[k]
 
 
@@ -56,6 +59,18 @@
     return mask, core
 
 
+def mixed_order(i):
+    first, last = 1 - (i + 15) // 16, i // 15
+    core = (1 - first) * (1 - last) * ((i + 1) % 2) + last
+    return (i + 1) // 2 - core * (1 - last) - last, core
+
+
+def mixed_mask(part, v):
+    code = v + (v + 5) // 8 - 2 * ((v + 4) // 8) + (v + 3) // 8
+    m1, m2, m3 = (BIT[axis] for axis in ORDER[part])
+    return (code % 2) * m1 + ((code // 2) % 2) * m2 + (code // 4) * m3
+
+
 def flip(bit, by):
     return bit + by - 2 * bit * by
 
@@ -80,8 +95,17 @@
         start = pl.multiple_of(block_of(i) * BLK, BLK)
         return pltpu.make_async_copy(a_hbm.at[:, pl.ds(start, BLK)], abuf.at[slot], asem.at[slot])
 
+    def load_mixed(i, slot):
+        v, other = mixed_order(i)
+        for part, (start, size) in enumerate(GATHER_COLS):
+            begin = pl.multiple_of(dev(mixed_mask(part, v), other) * BLK + start, 128)
+            pltpu.make_async_copy(a_hbm.at[:, pl.ds(begin, size)], abuf.at[slot, :, pl.ds(start, size)],
+                                  asem.at[slot]).start()
+
     def wait_a(slot):
         pltpu.make_async_copy(a_hbm.at[:, pl.ds(0, BLK)], abuf.at[slot], asem.at[slot]).wait()
+
+    twin = dev(0, 1)
 
     def remote(src, dst, send, recv, to):
         return pltpu.make_async_remote_copy(src_ref=src, dst_ref=dst, send_sem=send, recv_sem=recv,
@@ -100,23 +124,77 @@
     for load in loads:
         load.start()
     for i in range(RING):
-        load_a(i, i).start()
-    xall[me] = jnp.zeros((FROWS, BLK), BF16)
+        load_mixed(i, i)
+    xall[0] = jnp.zeros((FROWS, BLK), BF16)
     loads[0].wait()
-    xall[me, 0:FIN, :] = xin[...]
+    xall[0, 0:FIN, :] = xin[...]
     loads[1].wait()
     cnt[me] = jnp.full((1, 128), jnp.sum(m_ref[...].astype(F32)), F32)
     pl.semaphore_wait(barrier, 4)
 
+    def mixed_copy(axis, slot):
+        cols = pl.ds(*GATHER_COLS[gather_unit(axis, slot)[0]])
+        return remote(xall.at[SOURCE[slot], :, cols], xall.at[slot + 1, :, cols], snd.at[0], gr.at[slot], dev(BIT[axis]))
+
+    def mixed_start(*slots):
+        for slot in slots:
+            for axis in AXES:
+                mixed_copy(axis, slot).start()
+
+    def mixed_give(v):
+        remote(xall.at[v], xall.at[8 + v], snd.at[0], dr.at[v], twin).start()
+
+    def mixed_take(sems, n):
+        remote(xall.at[0], xall.at[0], snd.at[0], sems.at[n], me).wait_recv()
+
+    def mixed_product(i):
+        v, other = mixed_order(i)
+        return lax.dot_general(xall[8 * other + v], abuf[i % RING], NT, preferred_element_type=F32)
+
+    def mixed_refill(i):
+        @pl.when(i < NDEV - RING)
+        def _():
+            load_mixed(i + RING, i % RING)
+
+        @pl.when(i >= NDEV - RING)
+        def _():
+            load_a(i + RING - NDEV, i % RING).start()
+
+    def aggregate_features():
+        wait_a(0)
+        s1acc[0:FROWS, :] += mixed_product(0)
+        mixed_refill(0)
+
+        @pl.loop(0, 7)
+        def _(slot):
+            for k in range(7):
+                @pl.when(slot == k)
+                def _():
+                    mixed_take(gr, k)
+                    mixed_start(*(later for later in range(3, 7) if SOURCE[later] == k + 1))
+                    mixed_give(k + 1)
+            mixed_take(dr, slot)
+            i = 2 * slot + 1
+            wait_a(i % RING)
+            wait_a((i + 1) % RING)
+            s1acc[0:FROWS, :] += mixed_product(i) + mixed_product(i + 1)
+            mixed_refill(i)
+            mixed_refill(i + 1)
+
+        mixed_take(dr, 7)
+        wait_a((NDEV - 1) % RING)
+        s1acc[0:FROWS, :] += mixed_product(NDEV - 1)
+        mixed_refill(NDEV - 1)
+
     def gather(buf, g):
         def piece(owner, part):
-            return buf.at[owner, :, pl.ds(*GATHER_COLS[part])] if g == 0 else buf.at[owner, pl.ds(*GATHER_ROWS[part])]
+            return buf.at[owner, pl.ds(*GATHER_ROWS[part])]
 
         def copy(axis, slot):
             part, mask = gather_unit(axis, slot)
             ref = piece(dev(mask), part)
-            n = g * 11 + (slot if slot < 4 else 4 if slot == 6 else 2 * axis + slot + 1)
-            return remote(ref, ref, snd.at[g], gr.at[n], dev(1 << axis))
+            n = 7 + (slot if slot < 4 else 4 if slot == 6 else 2 * axis + slot + 1)
+            return remote(ref, ref, snd.at[g], gr.at[n], dev(BIT[axis]))
 
         def whole(sems, n):
             return remote(buf.at[me], buf.at[me], snd.at[g], sems.at[n], me)
@@ -124,33 +202,33 @@
         def give(*masks):
             for mask in masks:
                 owner = dev(mask)
-                for ref in [buf.at[owner]] if mask < 7 else [piece(owner, part) for part in range(3)]:
-                    remote(ref, ref, snd.at[g], dr.at[g * 8 + mask], dev(0, 1)).start()
+                for ref in [buf.at[owner]] if mask < 7 else [piece(owner, part) for part in AXES]:
+                    remote(ref, ref, snd.at[g], dr.at[8 + mask], twin).start()
 
         def take(*masks):
             for mask in masks:
-                whole(dr, g * 8 + mask).wait_recv()
+                whole(dr, 8 + mask).wait_recv()
 
         def begin():
-            for slot in range(3):
-                for axis in range(3):
+            for slot in AXES:
+                for axis in AXES:
                     copy(axis, slot).start()
             give(0)
 
         def forward(axis, slot, *onto):
             part, mask = gather_unit(axis, slot)
             for over, later in onto:
-                assert gather_unit(over, later) == (part, mask | (1 << axis))
+                assert gather_unit(over, later) == (part, mask | BIT[axis])
                 copy(over, later).start()
 
         def arrive(*slots):
             for slot in slots:
-                whole(gr, g * 11 + min(slot, 4)).wait_recv()
+                whole(gr, 7 + min(slot, 4)).wait_recv()
 
         def arrive_one(axis, slot):
             part, mask = gather_unit(axis, slot)
-            ref = piece(dev(mask | (1 << axis)), part)
-            remote(ref, ref, snd.at[g], gr.at[g * 11 + 2 * axis + slot + 1], me).wait_recv()
+            ref = piece(dev(mask | BIT[axis]), part)
+            remote(ref, ref, snd.at[g], gr.at[8 + 2 * axis + slot], me).wait_recv()
 
         def hooks(p):
             @pl.when(p == 0)
@@ -159,9 +237,9 @@
 
             @pl.when(p == 1)
             def _():
-                for slot in range(3):
+                for slot in AXES:
                     arrive(slot)
-                    for over in range(3):
+                    for over in AXES:
                         if slot == 0:
                             forward((over + 2) % 3, 0, (over, 3))
                         if slot == 1:
@@ -181,7 +259,7 @@
             @pl.when(p == 4)
             def _():
                 arrive(3)
-                for over in range(3):
+                for over in AXES:
                     forward((over + 2) % 3, 3, (over, 6))
                 arrive_one(1, 5)
                 arrive_one(0, 4)
@@ -210,45 +288,35 @@
             def _():
                 take(7)
 
-        def drain():
-            every = buf.at[pl.ds(0, 15)]
-            remote(every, every, snd.at[g], gr.at[g], me).wait_send()
-
-        return begin, hooks, tail, drain
-
-    def aggregate(buf, total, hooks, tail, g):
+        return begin, hooks, tail
+
+    def drain(buf, n):
+        every = buf.at[pl.ds(0, 15)]
+        remote(every, every, snd.at[n], gr.at[n], me).wait_send()
+
+    def aggregate(buf, total, hooks, tail):
         def product(i):
-            slot = (16 * g + i) % RING
-            if g == 0:
-                return lax.dot_general(buf[block_of(i)], abuf[slot], NT, preferred_element_type=F32)
-            return jnp.dot(abuf[slot], buf[block_of(i)], preferred_element_type=F32)
+            return jnp.dot(abuf[(NDEV + i) % RING], buf[block_of(i)], preferred_element_type=F32)
 
         def refill(i):
-            slot = (16 * g + i) % RING
-            if g == 0:
-                load_a((i + RING) % NDEV, slot).start()
-            else:
-                @pl.when(i < NDEV - RING)
-                def _():
-                    load_a(i + RING, slot).start()
-
-        rows = pl.ds(0, FROWS if g == 0 else BLK)
+            @pl.when(i < NDEV - RING)
+            def _():
+                load_a(i + RING, (NDEV + i) % RING).start()
 
         @pl.loop(0, 7)
         def _(p):
             hooks(p)
-            wait_a((16 * g + 2 * p) % RING)
-            wait_a((16 * g + 2 * p + 1) % RING)
-            total[rows, :] += product(2 * p) + product(2 * p + 1)
-            refill(2 * p)
-            refill(2 * p + 1)
+            for k in BOTH:
+                wait_a((NDEV + 2 * p + k) % RING)
+            total[...] += product(2 * p) + product(2 * p + 1)
+            for k in BOTH:
+                refill(2 * p + k)
 
         @pl.loop(0, 2)
         def _(k):
             tail(k)
-            wait_a((16 * g + 14 + k) % RING)
-            total[rows, :] += product(14 + k)
-            refill(14 + k)
+            wait_a((NDEV + 14 + k) % RING)
+            total[...] += product(14 + k)
 
     def small(x, src, dst, scatter=False):
         for d in far_first:
@@ -258,10 +326,10 @@
         ref = dst.at[pl.ds(0, 15)]
         remote(ref, ref, snd.at[3 + x], pr.at[x], me).wait()
 
-    begin_x, hooks_x, tail_x, drain_x = gather(xall, 0)
-    begin_h, hooks_h, tail_h, drain_h = gather(hall, 1)
-
-    begin_x()
+    begin_h, hooks_h, tail_h = gather(hall, 1)
+
+    mixed_start(0, 1, 2)
+    mixed_give(0)
     for load in loads[2:]:
         load.wait()
     w1p[...] = jnp.zeros_like(w1p)
@@ -271,7 +339,7 @@
     w2t[0:NCLS, :] = w2_ref[...].astype(BF16)
     s1acc[...] = jnp.zeros_like(s1acc)
     s2acc[...] = jnp.zeros_like(s2acc)
-    aggregate(xall, s1acc, hooks_x, tail_x, 0)
+    aggregate_features()
 
     s1b[...] = s1acc[...].astype(BF16)
     pre_one = jnp.dot(s1acc[...].T.astype(BF16), w1p[...].astype(BF16), preferred_element_type=F32)
@@ -279,7 +347,7 @@
     begin_h()
     small(0, cnt.at[me], cnt)
     z1t[...] = jnp.dot(w1t[...], s1b[...], preferred_element_type=F32)
-    aggregate(hall, s2acc, hooks_h, tail_h, 1)
+    aggregate(hall, s2acc, hooks_h, tail_h)
 
     small_wait(0, cnt)
     label_count = jnp.sum(cnt[...], axis=0)[0:1, 0:1]
@@ -299,18 +367,18 @@
 
     def pair_sum(mask, half=None):
         if half is None:
-            return remote(acc.at[8 + mask], drecv.at[mask], snd.at[2], er.at[mask], dev(0, 1))
+            return remote(acc.at[8 + mask], drecv.at[mask], snd.at[2], er.at[mask], twin)
         cols = pl.ds(half * 512, 512)
         return remote(acc.at[8 + mask, :, cols], drecv.at[mask, :, cols], snd.at[2], er.at[mask + half],
-                      dev(0, 1))
+                      twin)
 
     def unit_copy(part, k, half=None):
         axis, mask = reduce_unit(part, k)
         rows = pl.ds(*REDUCE_ROWS[part])
         if half is None:
-            return remote(acc.at[mask, rows], rbuf.at[k, rows], snd.at[2], rr.at[k], dev(1 << axis))
+            return remote(acc.at[mask, rows], rbuf.at[k, rows], snd.at[2], rr.at[k], dev(BIT[axis]))
         cols = pl.ds(half * 512, 512)
-        return remote(acc.at[mask, rows, cols], rbuf.at[k, rows, cols], snd.at[2], rr.at[k], dev(1 << axis))
+        return remote(acc.at[mask, rows, cols], rbuf.at[k, rows, cols], snd.at[2], rr.at[k], dev(BIT[axis]))
 
     def add_rows(mask, source, start, size, cols=slice(None)):
         @pl.loop(0, size // 8)
@@ -322,7 +390,7 @@
         pair_sum(mask).wait_recv()
         add_rows(mask, drecv.at[mask], 0, HID)
         for k in range(1, 4):
-            for part in range(3):
+            for part in AXES:
                 if reduce_unit(part, k)[1] == mask:
                     unit_copy(part, k).start()
 
@@ -331,18 +399,18 @@
         other, half = 1 - q // 2, q % 2
         cols = pl.ds(pl.multiple_of(half * 512, 512), 512)
         acc[7 + 8 * other, :, cols] = jnp.dot(ut[...], abuf[(30 + other) % RING, :, cols], preferred_element_type=F32)
-        for half in range(2):
+        for half in BOTH:
             @pl.when(q == half)
             def _():
                 pair_sum(7, half).start()
 
-    for j in range(2):
+    for j in BOTH:
         load_a(NDEV - 1 - j - RING, (31 - j) % RING).start()
 
     dw2_part = jnp.dot(gt[...], s2b[...], preferred_element_type=F32)
     d2src[...] = jnp.zeros_like(d2src)
     for j in range(6):
-        for k in range(2):
+        for k in BOTH:
             d2src[6 * k + j] = dw2_part[j * 8:(j + 1) * 8, k * 128:(k + 1) * 128]
     d2src[12] = jnp.full(TILE, loss_part, F32)
     d2src[13] = jnp.full(TILE, jnp.sum(weight), F32)
@@ -350,22 +418,22 @@
     d2r1[me] = d2src[me]
     small(1, d2src, d2r1, True)
 
-    for half in range(2):
+    for half in BOTH:
         pair_sum(7, half).wait_recv()
         add_rows(7, drecv.at[7], 0, HID, pl.ds(half * 512, 512))
-        for part in range(3):
+        for part in AXES:
             unit_copy(part, 0, half).start()
 
     @pl.loop(1, 8)
     def _(p):
-        for k in range(2):
+        for k in BOTH:
             @pl.when(p >= 3)
             def _():
                 wait_a((31 - 2 * p - k) % RING)
-        for k in range(2):
+        for k in BOTH:
             mask, other = step_order(NDEV - 1 - 2 * p - k)
             acc[mask + 8 * other] = jnp.dot(ut[...], abuf[(31 - 2 * p - k) % RING], preferred_element_type=F32)
-        for k in range(2):
+        for k in BOTH:
             @pl.when(p < 5)
             def _():
                 load_a(NDEV - 1 - 2 * p - k - RING, (31 - 2 * p - k) % RING).start()
@@ -385,9 +453,9 @@
 
     def take_units(k, send=None):
         units_wait(k)
-        for part in range(3):
+        for part in AXES:
             axis, mask = reduce_unit(part, k)
-            add_rows(mask - (1 << axis), rbuf.at[k], *REDUCE_ROWS[part])
+            add_rows(mask - BIT[axis], rbuf.at[k], *REDUCE_ROWS[part])
             if send is not None:
                 unit_copy(part, send).start()
 
@@ -406,9 +474,8 @@
     d1src[...] = lax.dot_general(grad_one, s1b[...], NT, preferred_element_type=F32).reshape(NDEV, 16, FPAD)
     d1r1[me] = d1src[me]
     small(3, d1src, d1r1, True)
-    drain_x()
-    drain_h()
-    remote(acc.at[pl.ds(0, 15)], acc.at[pl.ds(0, 15)], snd.at[2], pr.at[0], me).wait_send()
+    for n, buf in enumerate((xall, hall, acc)):
+        drain(buf, n)
     small_wait(2, d2out)
     keep_two.wait()
     small_wait(3, d1r1)
@@ -423,7 +490,7 @@
 def finish(d1_ref, d2_ref, loss_out, dw1_out, dw2_out):
     loss_out[...] = d2_ref[12, 0:1, 0:1] / d2_ref[13, 0:1, 0:1]
     dw1_out[...] = d1_ref[...].reshape(HID, FPAD).T[0:FIN, :]
-    for k in range(2):
+    for k in BOTH:
         dw2_out[:, pl.ds(k * 128, 128)] = d2_ref[pl.ds(6 * k, 6)].reshape(CPAD, 128)[0:NCLS]
 
 
@@ -464,7 +531,7 @@
                 pltpu.VMEM(TILE, F32),
                 *[pltpu.VMEM((NDEV, 16, FPAD), F32)] * 2,
                 pltpu.VMEM((16, FPAD), F32),
-                *[dma((n,)) for n in (RING, 5, 22, 16, 7, 9, 5, 8)],
+                *[dma((n,)) for n in (RING, 5, 18, 16, 7, 9, 5, 8)],
             ],
             compiler_params=pltpu.CompilerParams(collective_id=0, has_side_effects=True,
                                                  vmem_limit_bytes=67 * 1000 * 1000),

time: 127 us -> 126 us (level)
  no operation moved by 1% of the time
where the time goes in v6:
time: 126 us
  Pallas kernels  126 us (100%)
    pallas_call x1, Pallas kernels, local_step(): pl.pallas_call(kernel, out_shape=(jax.ShapeDtypeStruct((NDEV, 16, FPAD),...  124 us

profile of v6, /device:TPU:0, one launch (start us, length us, event | category | flops | bytes accessed | tf_op | source)
XLA Modules:
  0.0 126.2 jit_solution(608130149816148152)
XLA Ops:
  0.6 123.9 %shard_map.85 = (f32[16,16,128]{2,1,0:T(8,128)}, f32[16,8,128]{2,1,0:T(8,128)}) custom-call(bf16[1024,16384]{1,0:T(8,128)(2,1)} %a_hbm.1, bf16[100,1024]{1,0:T(8,128)(2,1)} %bitcast.6, f32[100,256]{1,0:T(8,128)} %w1_hbm.1, f32[47,256]{1,0:T(8,128)} %bitcast.7, s32[1,1024]{1,0:T(1,128)} %bitcast.8, s32[1,1024]{1,0:T(1,128)} %bitcast.9), custom_call_target="tpu_custom_call" | custom-call | tf_op jit(solution)/shard_map/pallas_call | solution.py:502
  124.6 1.7 %shard_map.86 = (f32[1,1]{1,0:T(1,128)}, f32[100,256]{1,0:T(8,128)}, f32[47,256]{1,0:T(8,128)}) custom-call(f32[16,16,128]{2,1,0:T(8,128)} %get-tuple-element.8.d1_ref, f32[16,8,128]{2,1,0:T(8,128)} %get-tuple-element.9.d2_ref), custom_call_target="tpu_custom_call" | custom-call | tf_op jit(solution)/shard_map/pallas_call | solution.py:539

commit v7 on v6

--- a/solution.py
+++ b/solution.py
@@ -20,28 +20,24 @@
 
 AXES, BOTH = range(3), range(2)
 BIT = (1, 2, 4)
-SOURCE = (0, 0, 0, 1, 1, 2, 4)
 ORDER = tuple((p, (p + 1) % 3, (p + 2) % 3) for p in AXES)
 GATHER_ROWS = ((0, 352), (352, 336), (688, 336))
-GATHER_COLS = ((0, 384), (384, 384), (768, 256))
+MIXED_ORDER = (*ORDER, (0, 2, 1))
+MIXED_COLS = ((0, 256), (256, 384), (640, 256), (896, 128))
 REDUCE_ROWS = ((0, 88), (88, 88), (176, 80))
 
 NT = (((1,), (1,)), ((), ()))
 TN = (((0,), (0,)), ((), ()))
 
 
+CODE = (0, 1, 2, 4, 3, 5, 6, 7)
+VIA = [code.bit_length() - 1 for code in CODE[1:]]
+SOURCE = [CODE.index(code - (1 << via)) for code, via in zip(CODE[1:], VIA)]
+
+
 def gather_unit(axis, slot):
-    first, second, third = axis, (axis + 2) % 3, (axis + 1) % 3
-    if slot == 0:
-        return first, 0
-    if slot == 1:
-        return second, 0
-    if slot == 2:
-        return third, 0
-    if slot == 3:
-        return second, 1 << ORDER[second][0]
-    one, two = 1 << ORDER[third][0], 1 << ORDER[third][1]
-    return third, {4: one, 5: two, 6: one | two}[slot]
+    part = next(p for p in AXES if ORDER[p][VIA[slot]] == axis)
+    return part, sum(BIT[ORDER[part][j]] for j in AXES if CODE[SOURCE[slot]] >> j & 1)
 
 
 def reduce_unit(part, k):
@@ -67,7 +63,7 @@
 
 def mixed_mask(part, v):
     code = v + (v + 5) // 8 - 2 * ((v + 4) // 8) + (v + 3) // 8
-    m1, m2, m3 = (BIT[axis] for axis in ORDER[part])
+    m1, m2, m3 = (BIT[axis] for axis in MIXED_ORDER[part])
     return (code % 2) * m1 + ((code // 2) % 2) * m2 + (code // 4) * m3
 
 
@@ -97,7 +93,7 @@
 
     def load_mixed(i, slot):
         v, other = mixed_order(i)
-        for part, (start, size) in enumerate(GATHER_COLS):
+        for part, (start, size) in enumerate(MIXED_COLS):
             begin = pl.multiple_of(dev(mixed_mask(part, v), other) * BLK + start, 128)
             pltpu.make_async_copy(a_hbm.at[:, pl.ds(begin, size)], abuf.at[slot, :, pl.ds(start, size)],
                                   asem.at[slot]).start()
@@ -132,14 +128,14 @@
     cnt[me] = jnp.full((1, 128), jnp.sum(m_ref[...].astype(F32)), F32)
     pl.semaphore_wait(barrier, 4)
 
-    def mixed_copy(axis, slot):
-        cols = pl.ds(*GATHER_COLS[gather_unit(axis, slot)[0]])
+    def mixed_copy(part, slot):
+        axis, cols = MIXED_ORDER[part][VIA[slot]], pl.ds(*MIXED_COLS[part])
         return remote(xall.at[SOURCE[slot], :, cols], xall.at[slot + 1, :, cols], snd.at[0], gr.at[slot], dev(BIT[axis]))
 
     def mixed_start(*slots):
         for slot in slots:
-            for axis in AXES:
-                mixed_copy(axis, slot).start()
+            for part in range(4):
+                mixed_copy(part, slot).start()
 
     def mixed_give(v):
         remote(xall.at[v], xall.at[8 + v], snd.at[0], dr.at[v], twin).start()
@@ -407,6 +403,52 @@
     for j in BOTH:
         load_a(NDEV - 1 - j - RING, (31 - j) % RING).start()
 
+    for half in BOTH:
+        pair_sum(7, half).wait_recv()
+        add_rows(7, drecv.at[7], 0, HID, pl.ds(half * 512, 512))
+        for part in AXES:
+            unit_copy(part, 0, half).start()
+
+    @pl.loop(1, 8)
+    def _(p):
+        for k in BOTH:
+            @pl.when(p >= 3)
+            def _():
+                wait_a((31 - 2 * p - k) % RING)
+        for k in BOTH:
+            mask, other = step_order(NDEV - 1 - 2 * p - k)
+            acc[mask + 8 * other] = jnp.dot(ut[...], abuf[(31 - 2 * p - k) % RING], preferred_element_type=F32)
+        for k in BOTH:
+            @pl.when(p < 5)
+            def _():
+                load_a(NDEV - 1 - 2 * p - k - RING, (31 - 2 * p - k) % RING).start()
+
+        for step in range(2, NDEV):
+            step_mask, step_other = step_order(NDEV - 1 - step)
+
+            @pl.when(p == step // 2)
+            def _():
+                if step_other:
+                    pair_sum(step_mask).start()
+                else:
+                    take_pair(step_mask)
+
+    def units_wait(k):
+        remote(rbuf.at[k], rbuf.at[k], snd.at[2], rr.at[k], me).wait_recv()
+
+    def take_units(k, send=None):
+        units_wait(k)
+        for part in AXES:
+            axis, mask = reduce_unit(part, k)
+            add_rows(mask - BIT[axis], rbuf.at[k], *REDUCE_ROWS[part])
+            if send is not None:
+                unit_copy(part, send).start()
+
+    take_units(0, 4)
+    take_units(1, 5)
+    take_units(2)
+    take_units(3)
+    take_units(4, 6)
     dw2_part = jnp.dot(gt[...], s2b[...], preferred_element_type=F32)
     d2src[...] = jnp.zeros_like(d2src)
     for j in range(6):
@@ -417,72 +459,25 @@
     keep_two = pltpu.make_async_copy(d2r2, d2out.at[me], xsem.at[0])
     d2r1[me] = d2src[me]
     small(1, d2src, d2r1, True)
-
-    for half in BOTH:
-        pair_sum(7, half).wait_recv()
-        add_rows(7, drecv.at[7], 0, HID, pl.ds(half * 512, 512))
-        for part in AXES:
-            unit_copy(part, 0, half).start()
-
-    @pl.loop(1, 8)
-    def _(p):
-        for k in BOTH:
-            @pl.when(p >= 3)
-            def _():
-                wait_a((31 - 2 * p - k) % RING)
-        for k in BOTH:
-            mask, other = step_order(NDEV - 1 - 2 * p - k)
-            acc[mask + 8 * other] = jnp.dot(ut[...], abuf[(31 - 2 * p - k) % RING], preferred_element_type=F32)
-        for k in BOTH:
-            @pl.when(p < 5)
-            def _():
-                load_a(NDEV - 1 - 2 * p - k - RING, (31 - 2 * p - k) % RING).start()
-
-        for step in range(2, NDEV):
-            step_mask, step_other = step_order(NDEV - 1 - step)
-
-            @pl.when(p == step // 2)
-            def _():
-                if step_other:
-                    pair_sum(step_mask).start()
-                else:
-                    take_pair(step_mask)
-
-    def units_wait(k):
-        remote(rbuf.at[k], rbuf.at[k], snd.at[2], rr.at[k], me).wait_recv()
-
-    def take_units(k, send=None):
-        units_wait(k)
-        for part in AXES:
-            axis, mask = reduce_unit(part, k)
-            add_rows(mask - BIT[axis], rbuf.at[k], *REDUCE_ROWS[part])
-            if send is not None:
-                unit_copy(part, send).start()
-
-    take_units(0, 4)
-    take_units(1, 5)
-    take_units(2)
-    small_wait(1, d2r1)
-    d2r2[...] = jnp.sum(d2r1[...], axis=0)
-    take_units(3)
-    take_units(4, 6)
-    small(2, d2r2, d2out)
-    keep_two.start()
     take_units(5)
     units_wait(6)
     grad_one = jnp.where(z1t[...] > 0.0, acc[0] + rbuf[6], 0.0).astype(BF16)
     d1src[...] = lax.dot_general(grad_one, s1b[...], NT, preferred_element_type=F32).reshape(NDEV, 16, FPAD)
     d1r1[me] = d1src[me]
     small(3, d1src, d1r1, True)
+    small_wait(1, d2r1)
+    d2r2[...] = jnp.sum(d2r1[...], axis=0)
+    small(2, d2r2, d2out)
+    keep_two.start()
     for n, buf in enumerate((xall, hall, acc)):
         drain(buf, n)
-    small_wait(2, d2out)
-    keep_two.wait()
     small_wait(3, d1r1)
     d1r2[...] = jnp.sum(d1r1[...], axis=0)
     small(4, d1r2, d1out)
     keep_one = pltpu.make_async_copy(d1r2, d1out.at[me], xsem.at[1])
     keep_one.start()
+    small_wait(2, d2out)
+    keep_two.wait()
     keep_one.wait()
     small_wait(4, d1out)
 

time: 126 us -> 127 us (level)
  no operation moved by 1% of the time
where the time goes in v7:
time: 127 us
  Pallas kernels  126 us (99%)
    pallas_call x1, Pallas kernels, local_step(): pl.pallas_call(kernel, out_shape=(jax.ShapeDtypeStruct((NDEV, 16, FPAD),...  124 us

profile of v7, /device:TPU:0, one launch (start us, length us, event | category | flops | bytes accessed | tf_op | source)
XLA Modules:
  0.0 126.5 jit_solution(7569691344208758474)
XLA Ops:
  0.6 124.2 %shard_map.85 = (f32[16,16,128]{2,1,0:T(8,128)}, f32[16,8,128]{2,1,0:T(8,128)}) custom-call(bf16[1024,16384]{1,0:T(8,128)(2,1)} %a_hbm.1, bf16[100,1024]{1,0:T(8,128)(2,1)} %bitcast.6, f32[100,256]{1,0:T(8,128)} %w1_hbm.1, f32[47,256]{1,0:T(8,128)} %bitcast.7, s32[1,1024]{1,0:T(1,128)} %bitcast.8, s32[1,1024]{1,0:T(1,128)} %bitcast.9), custom_call_target="tpu_custom_call" | custom-call | tf_op jit(solution)/shard_map/pallas_call | solution.py:497
  124.8 1.7 %shard_map.86 = (f32[1,1]{1,0:T(1,128)}, f32[100,256]{1,0:T(8,128)}, f32[47,256]{1,0:T(8,128)}) custom-call(f32[16,16,128]{2,1,0:T(8,128)} %get-tuple-element.8.d1_ref, f32[16,8,128]{2,1,0:T(8,128)} %get-tuple-element.9.d2_ref), custom_call_target="tpu_custom_call" | custom-call | tf_op jit(solution)/shard_map/pallas_call | solution.py:534

commit v8 on v7

--- a/solution.py
+++ b/solution.py
@@ -18,12 +18,11 @@
 RING = 6
 TILE = (8, 128)
 
-AXES, BOTH = range(3), range(2)
+AXES, BOTH, QUARTERS = range(3), range(2), range(4)
 BIT = (1, 2, 4)
 ORDER = tuple((p, (p + 1) % 3, (p + 2) % 3) for p in AXES)
 GATHER_ROWS = ((0, 352), (352, 336), (688, 336))
-MIXED_ORDER = (*ORDER, (0, 2, 1))
-MIXED_COLS = ((0, 256), (256, 384), (640, 256), (896, 128))
+MIXED_COLS = ((0, 384), (384, 384), (768, 256))
 REDUCE_ROWS = ((0, 88), (88, 88), (176, 80))
 
 NT = (((1,), (1,)), ((), ()))
@@ -63,7 +62,7 @@
 
 def mixed_mask(part, v):
     code = v + (v + 5) // 8 - 2 * ((v + 4) // 8) + (v + 3) // 8
-    m1, m2, m3 = (BIT[axis] for axis in MIXED_ORDER[part])
+    m1, m2, m3 = (BIT[axis] for axis in ORDER[part])
     return (code % 2) * m1 + ((code // 2) % 2) * m2 + (code // 4) * m3
 
 
@@ -129,12 +128,12 @@
     pl.semaphore_wait(barrier, 4)
 
     def mixed_copy(part, slot):
-        axis, cols = MIXED_ORDER[part][VIA[slot]], pl.ds(*MIXED_COLS[part])
+        axis, cols = ORDER[part][VIA[slot]], pl.ds(*MIXED_COLS[part])
         return remote(xall.at[SOURCE[slot], :, cols], xall.at[slot + 1, :, cols], snd.at[0], gr.at[slot], dev(BIT[axis]))
 
     def mixed_start(*slots):
         for slot in slots:
-            for part in range(4):
+            for part in AXES:
                 mixed_copy(part, slot).start()
 
     def mixed_give(v):
@@ -361,19 +360,19 @@
     gt[...] = grad.astype(BF16)
     ut[...] = lax.dot_general(w2t[...], gt[...], TN, preferred_element_type=F32).astype(BF16)
 
-    def pair_sum(mask, half=None):
-        if half is None:
+    def pair_sum(mask, quarter=None):
+        if quarter is None:
             return remote(acc.at[8 + mask], drecv.at[mask], snd.at[2], er.at[mask], twin)
-        cols = pl.ds(half * 512, 512)
-        return remote(acc.at[8 + mask, :, cols], drecv.at[mask, :, cols], snd.at[2], er.at[mask + half],
+        cols = pl.ds(quarter * 256, 256)
+        return remote(acc.at[8 + mask, :, cols], drecv.at[mask, :, cols], snd.at[2], er.at[mask + quarter],
                       twin)
 
-    def unit_copy(part, k, half=None):
+    def unit_copy(part, k, quarter=None):
         axis, mask = reduce_unit(part, k)
         rows = pl.ds(*REDUCE_ROWS[part])
-        if half is None:
+        if quarter is None:
             return remote(acc.at[mask, rows], rbuf.at[k, rows], snd.at[2], rr.at[k], dev(BIT[axis]))
-        cols = pl.ds(half * 512, 512)
+        cols = pl.ds(quarter * 256, 256)
         return remote(acc.at[mask, rows, cols], rbuf.at[k, rows, cols], snd.at[2], rr.at[k], dev(BIT[axis]))
 
     def add_rows(mask, source, start, size, cols=slice(None)):
@@ -390,24 +389,23 @@
                 if reduce_unit(part, k)[1] == mask:
                     unit_copy(part, k).start()
 
-    @pl.loop(0, 4)
-    def _(q):
-        other, half = 1 - q // 2, q % 2
-        cols = pl.ds(pl.multiple_of(half * 512, 512), 512)
-        acc[7 + 8 * other, :, cols] = jnp.dot(ut[...], abuf[(30 + other) % RING, :, cols], preferred_element_type=F32)
-        for half in BOTH:
-            @pl.when(q == half)
-            def _():
-                pair_sum(7, half).start()
+    for other in (1, 0):
+        for q in QUARTERS:
+            cols = pl.ds(q * 256, 256)
+            acc[7 + 8 * other, :, cols] = jnp.dot(ut[...], abuf[(30 + other) % RING, :, cols],
+                                                  preferred_element_type=F32)
+            if other:
+                pair_sum(7, q).start()
 
     for j in BOTH:
         load_a(NDEV - 1 - j - RING, (31 - j) % RING).start()
 
-    for half in BOTH:
-        pair_sum(7, half).wait_recv()
-        add_rows(7, drecv.at[7], 0, HID, pl.ds(half * 512, 512))
+    for q in QUARTERS:
+        pair_sum(7, q).wait_recv()
+        cols = pl.ds(q * 256, 256)
+        acc[7, :, cols] += drecv[7, :, cols]
         for part in AXES:
-            unit_copy(part, 0, half).start()
+            unit_copy(part, 0, q).start()
 
     @pl.loop(1, 8)
     def _(p):
@@ -526,7 +524,7 @@
                 pltpu.VMEM(TILE, F32),
                 *[pltpu.VMEM((NDEV, 16, FPAD), F32)] * 2,
                 pltpu.VMEM((16, FPAD), F32),
-                *[dma((n,)) for n in (RING, 5, 18, 16, 7, 9, 5, 8)],
+                *[dma((n,)) for n in (RING, 5, 18, 16, 7, 11, 5, 8)],
             ],
             compiler_params=pltpu.CompilerParams(collective_id=0, has_side_effects=True,
                                                  vmem_limit_bytes=67 * 1000 * 1000),

time: 127 us -> 126 us (level)
  no operation moved by 1% of the time
where the time goes in v8:
time: 126 us; the launch traced here: 125 us
  Pallas kernels  125 us (99%)
    pallas_call x1, Pallas kernels, local_step(): pl.pallas_call(kernel, out_shape=(jax.ShapeDtypeStruct((NDEV, 16, FPAD),...  123 us

profile of v8, /device:TPU:0, one launch (start us, length us, event | category | flops | bytes accessed | tf_op | source)
XLA Modules:
  0.0 125.4 jit_solution(4418027397772366173)
XLA Ops:
  0.6 123.1 %shard_map.85 = (f32[16,16,128]{2,1,0:T(8,128)}, f32[16,8,128]{2,1,0:T(8,128)}) custom-call(bf16[1024,16384]{1,0:T(8,128)(2,1)} %a_hbm.1, bf16[100,1024]{1,0:T(8,128)(2,1)} %bitcast.6, f32[100,256]{1,0:T(8,128)} %w1_hbm.1, f32[47,256]{1,0:T(8,128)} %bitcast.7, s32[1,1024]{1,0:T(1,128)} %bitcast.8, s32[1,1024]{1,0:T(1,128)} %bitcast.9), custom_call_target="tpu_custom_call" | custom-call | tf_op jit(solution)/shard_map/pallas_call | solution.py:495
  123.7 1.7 %shard_map.86 = (f32[1,1]{1,0:T(1,128)}, f32[100,256]{1,0:T(8,128)}, f32[47,256]{1,0:T(8,128)}) custom-call(f32[16,16,128]{2,1,0:T(8,128)} %get-tuple-element.8.d1_ref, f32[16,8,128]{2,1,0:T(8,128)} %get-tuple-element.9.d2_ref), custom_call_target="tpu_custom_call" | custom-call | tf_op jit(solution)/shard_map/pallas_call | solution.py:532

commit v9 on v8

--- a/solution.py
+++ b/solution.py
@@ -274,14 +274,11 @@
                 take(5, 6)
 
         def tail(i):
-            @pl.when(i == 0)
-            def _():
+            if i:
+                take(7)
+            else:
                 arrive(6)
                 give(7)
-
-            @pl.when(i == 1)
-            def _():
-                take(7)
 
         return begin, hooks, tail
 
@@ -307,11 +304,13 @@
             for k in BOTH:
                 refill(2 * p + k)
 
-        @pl.loop(0, 2)
-        def _(k):
+        for k in BOTH:
             tail(k)
             wait_a((NDEV + 14 + k) % RING)
-            total[...] += product(14 + k)
+            result = total[...] + product(14 + k)
+            if k:
+                return result
+            total[...] = result
 
     def small(x, src, dst, scatter=False):
         for d in far_first:
@@ -342,11 +341,10 @@
     begin_h()
     small(0, cnt.at[me], cnt)
     z1t[...] = jnp.dot(w1t[...], s1b[...], preferred_element_type=F32)
-    aggregate(hall, s2acc, hooks_h, tail_h)
+    s2b[...] = aggregate(hall, s2acc, hooks_h, tail_h).astype(BF16)
 
     small_wait(0, cnt)
     label_count = jnp.sum(cnt[...], axis=0)[0:1, 0:1]
-    s2b[...] = s2acc[...].astype(BF16)
     logits = lax.dot_general(w2t[...], s2b[...], NT, preferred_element_type=F32)
     classes = lax.broadcasted_iota(jnp.int32, (CPAD, BLK), 0)
     logits = jnp.where(classes < NCLS, logits, -jnp.inf)

time: 126 us -> 126 us (level)
  no operation moved by 1% of the time
where the time goes in v9:
time: 126 us
  Pallas kernels  126 us (100%)
    pallas_call x1, Pallas kernels, local_step(): pl.pallas_call(kernel, out_shape=(jax.ShapeDtypeStruct((NDEV, 16, FPAD),...  124 us

profile of v9, /device:TPU:0, one launch (start us, length us, event | category | flops | bytes accessed | tf_op | source)
XLA Modules:
  0.0 126.2 jit_solution(7061316666592350313)
XLA Ops:
  0.6 123.9 %shard_map.85 = (f32[16,16,128]{2,1,0:T(8,128)}, f32[16,8,128]{2,1,0:T(8,128)}) custom-call(bf16[1024,16384]{1,0:T(8,128)(2,1)} %a_hbm.1, bf16[100,1024]{1,0:T(8,128)(2,1)} %bitcast.6, f32[100,256]{1,0:T(8,128)} %w1_hbm.1, f32[47,256]{1,0:T(8,128)} %bitcast.7, s32[1,1024]{1,0:T(1,128)} %bitcast.8, s32[1,1024]{1,0:T(1,128)} %bitcast.9), custom_call_target="tpu_custom_call" | custom-call | tf_op jit(solution)/shard_map/pallas_call | solution.py:493
  124.5 1.7 %shard_map.86 = (f32[1,1]{1,0:T(1,128)}, f32[100,256]{1,0:T(8,128)}, f32[47,256]{1,0:T(8,128)}) custom-call(f32[16,16,128]{2,1,0:T(8,128)} %get-tuple-element.8.d1_ref, f32[16,8,128]{2,1,0:T(8,128)} %get-tuple-element.9.d2_ref), custom_call_target="tpu_custom_call" | custom-call | tf_op jit(solution)/shard_map/pallas_call | solution.py:530
